TPU v7x, 32 devices: a whole 2x2x4 slice. The times are simulated.
32 devices in a mesh: mem: 4 (over y, core), tile: 8 (over z, x).
Axes of the slice: x: 2, y: 2, z: 4, core: 2. Of those that a mesh axis runs over, the one named last changes fastest.
Arguments:
- ensemble_profiles_before: bfloat16 [64, 40, 4096], P('mem', None, 'tile'), may hold values from -6 to 6
- mixing_coefficient: float32 [4096], P('tile'), may hold values from 0.05 to 0.24
- surface_driver: float32 [64, 4096], P('mem', 'tile'), may hold values from -3 to 3
- terrain_indicator: int32 [4096], P('tile'), may hold values 0 or 1
- measured_profile_position: int32 [32768], P('tile'), may hold values from 0 to 511
- measured_field_index: int32 [32768], P('tile'), may hold values from 0 to 39
- obs_valid: int32 [32768], P('tile'), may hold values 0 or 1
- obs_value: bfloat16 [32768], P('tile'), may hold values from -6 to 6
- obs_error: bfloat16 [32768], P('tile'), may hold values from 0.5 to 4
- local_weight: float32 [4, 8, 20480], P('mem', 'tile'), may hold values from 0.001 to 0.03
Outputs:
- analysis: bfloat16 [64, 40, 4096], P('mem', None, 'tile')
All inputs are finite; a program needn't handle non-finite values. No bound on the sum of `terrain_indicator` or of `obs_valid` on one device may be relied on, other than what follows from the above.
Results may differ from a plain program's by a relative error of at most 0.0034.
Values may be sent and summed in bfloat16 or wider, within the bound.
A program may use at most 64 MiB of HBM per device.

v0:
```python
import functools

import jax
import jax.numpy as jnp
from jax import lax
from jax.experimental import pallas as pl
from jax.experimental.pallas import tpu as pltpu
from jax.sharding import PartitionSpec as P

REACH = 2
NS_ITERS = 3


EXACT = lax.Precision.HIGHEST


def from_behind(value, axis, steps):
    count = lax.axis_size(axis)
    pairs = [(source, (source + steps) % count) for source in range(count)]
    return lax.ppermute(value, axis, pairs)


def vertical_mixing_step(
    ensemble_profiles_before, mixing_coefficient, surface_driver, terrain_indicator
):
    values = ensemble_profiles_before.astype(jnp.float32)
    above_layer = jnp.concatenate([values[:, :1], values[:, :-1]], axis=1)
    below_layer = jnp.concatenate([values[:, 1:], values[:, -1:]], axis=1)
    diffused = values + mixing_coefficient[None, None, :] * (
        above_layer - 2.0 * values + below_layer
    )
    stepped = diffused - 0.05 * values * values * values
    surface = jnp.concatenate([stepped[:, :1] + surface_driver[:, None, :], stepped[:, 1:]], axis=1)
    result = jnp.where(terrain_indicator[None, None, :] > 0, surface, values)
    return result.astype(jnp.bfloat16)


def measurement_operator(background_ensemble, measured_profile_position, measured_field_index):
    profile_sequence = background_ensemble.shape[2]
    unrolled_ensemble = background_ensemble.reshape(background_ensemble.shape[0], -1)
    slot_index = measured_field_index * profile_sequence + measured_profile_position
    return jnp.take(unrolled_ensemble, slot_index, axis=1)


def prepare(window):
    ensemble_profiles = window.shape[0] - 3
    measured_quantities = window[:ensemble_profiles].astype(jnp.float32)
    average = jnp.mean(measured_quantities, axis=0)
    deviation = measured_quantities - average
    innovation = window[ensemble_profiles].astype(jnp.float32) - average
    obs_precision = window[ensemble_profiles + 2].astype(jnp.float32) / window[
        ensemble_profiles + 1
    ].astype(jnp.float32)
    return (deviation, innovation, obs_precision)


def weights_for(deviation, innovation, precision, portions):
    ensemble_profiles = deviation.shape[0]
    portion_width = deviation.shape[1] // portions
    spread = jnp.zeros((ensemble_profiles, ensemble_profiles), jnp.float32)
    for portion_index in range(portions):
        portion = deviation[:, portion_index * portion_width : (portion_index + 1) * portion_width]
        scaled = (
            portion
            * precision[None, portion_index * portion_width : (portion_index + 1) * portion_width]
        )
        spread = spread + jnp.dot(
            scaled, portion.T, precision=EXACT, preferred_element_type=jnp.float32
        )
    spread = spread / (ensemble_profiles - 1.0)
    pulled = jnp.dot(
        deviation, precision * innovation, precision=EXACT, preferred_element_type=jnp.float32
    ) / (ensemble_profiles - 1.0)
    identity = jnp.eye(ensemble_profiles, dtype=jnp.float32)
    system = identity + spread
    norm_scale = jnp.sqrt(jnp.sum(system * system))

    def newton(sweep, carry):
        current, inv_root = carry
        middle = 1.5 * identity - 0.5 * jnp.dot(inv_root, current, precision=EXACT)
        return (
            jnp.dot(current, middle, precision=EXACT),
            jnp.dot(middle, inv_root, precision=EXACT),
        )

    current, inv_root = lax.fori_loop(0, NS_ITERS, newton, (system / norm_scale, identity))
    inv_root = inv_root / jnp.sqrt(norm_scale)
    inverse = jnp.dot(inv_root, inv_root, precision=EXACT)
    mean_weight = jnp.dot(inverse, pulled, precision=EXACT)
    return inv_root + mean_weight[:, None]


def update(states, transform, land_block):
    values = states.astype(jnp.float32)
    average = jnp.mean(values, axis=0)
    deviation = values - average[None]
    moved = jnp.einsum("isc,ij->jsc", deviation, transform, precision=EXACT)
    result = jnp.where(land_block[None, None, :] > 0, average[None] + moved, values)
    return result.astype(jnp.bfloat16)


def plain_on_device(
    ensemble_profiles_before,
    mixing_coefficient,
    surface_driver,
    terrain_indicator,
    measured_profile_position,
    measured_field_index,
    obs_valid,
    obs_value,
    obs_error,
    local_weight,
):
    background_ensemble = vertical_mixing_step(
        ensemble_profiles_before, mixing_coefficient, surface_driver, terrain_indicator
    )
    measured_quantities = measurement_operator(
        background_ensemble, measured_profile_position, measured_field_index
    )
    metadata = jnp.stack([obs_value, obs_error, obs_valid.astype(jnp.bfloat16)])
    own_rows = jnp.concatenate([measured_quantities, metadata], axis=0)
    pieces = []
    for offset in range(-REACH, REACH + 1):
        if offset == 0:
            pieces.append(own_rows)
        else:
            pieces.append(from_behind(own_rows, "tile", -offset))
    nearby = jnp.concatenate(pieces, axis=1)
    members_here = measured_quantities.shape[0]
    everyone = lax.all_gather(nearby[:members_here], "mem", axis=0, tiled=True)
    window = jnp.concatenate([everyone, nearby[members_here:]], axis=0)
    regrouped_states = lax.all_to_all(
        background_ensemble, "mem", split_axis=2, concat_axis=0, tiled=True
    )
    deviation, innovation, obs_precision = prepare(window)
    columns_here = regrouped_states.shape[2]
    local_land = lax.dynamic_slice_in_dim(
        terrain_indicator, lax.axis_index("mem") * columns_here, columns_here
    )
    transform = weights_for(
        deviation, innovation, obs_precision * local_weight[0, 0], 2 * REACH + 1
    )
    outputs = update(regrouped_states, transform, local_land)
    return lax.all_to_all(outputs, "mem", split_axis=0, concat_axis=2, tiled=True)


MESH = pl.DeviceIdType.MESH
HALVES = 2
FIELD_CUTS = (0.25, 0.5, 0.8)
CORES = 2


def exact_dot(a, b):
    return jnp.dot(a, b, precision=EXACT, preferred_element_type=jnp.float32)


def kernel(
    n_mem,
    n_tile,
    cuts,
    ens_hbm,
    mix_hbm,
    surf_hbm,
    land_hbm,
    pos_hbm,
    field_hbm,
    valid_hbm,
    value_hbm,
    error_hbm,
    weight_hbm,
    out_ref,
    ens_ref,
    mix_ref,
    surf_ref,
    land_ref,
    pos_ref,
    field_ref,
    valid_ref,
    value_ref,
    error_ref,
    fc_ref,
    seen_ref,
    near_ref,
    slot_ref,
    acc_ref,
    part_ref,
    got_ref,
    tsend_ref,
    trecv_ref,
    moved_ref,
    ens_sem,
    in_sem,
    seen_send,
    seen_recv,
    fc_send,
    fc_recv,
    w_send,
    w_recv,
    p_send,
    p_recv,
    t_send,
    t_recv,
):
    members, fields, columns = ens_ref.shape
    everyone = members * n_mem
    slots = pos_ref.shape[1]
    near = 2 * REACH + 1
    me, tile = lax.axis_index("mem"), lax.axis_index("tile")
    n_y = n_mem // CORES
    y, core = me // CORES, lax.rem(me, CORES)
    sibling = y * CORES + (1 - core)
    across = [lax.rem(y + step, n_y) * CORES + core for step in range(1, n_y)]
    partner_of = [lax.rem(y + step, n_y) * CORES + (1 - core) for step in range(1, n_y)]

    barrier = pltpu.get_barrier_semaphore()
    for step in range(1, n_mem):
        pl.semaphore_signal(
            barrier, inc=1, device_id={"mem": lax.rem(me + step, n_mem)}, device_id_type=MESH
        )
    for offset in range(-REACH, REACH + 1):
        if offset:
            pl.semaphore_signal(
                barrier,
                inc=1,
                device_id={"tile": lax.rem(tile + offset + n_tile, n_tile)},
                device_id_type=MESH,
            )

    lanes = 128

    def ens_copy(step):
        where = pl.ds(pl.multiple_of(step * lanes, lanes), lanes)
        return pltpu.make_async_copy(
            ens_hbm.at[:, :, where], ens_ref.at[:, :, where], ens_sem.at[step]
        )

    pairs = [
        (mix_hbm, mix_ref),
        (surf_hbm, surf_ref),
        (land_hbm, land_ref),
        (pos_hbm, pos_ref),
        (field_hbm, field_ref),
        (valid_hbm, valid_ref),
        (value_hbm, value_ref),
        (error_hbm, error_ref),
        (weight_hbm.at[REACH], near_ref.at[REACH]),
    ]
    inputs = [
        pltpu.make_async_copy(src, dst, in_sem.at[index]) for index, (src, dst) in enumerate(pairs)
    ]
    for copy in inputs[:3]:
        copy.start()
    for step in range(columns // lanes):
        ens_copy(step).start()
    for copy in inputs[3:]:
        copy.start()
    for copy in inputs[:3]:
        copy.wait()

    def mix(step, carry):
        where = pl.ds(pl.multiple_of(step * lanes, lanes), lanes)
        ens_copy(step).wait()
        x = jnp.transpose(ens_ref[:, :, where].astype(jnp.float32), (1, 0, 2))
        rate = mix_ref[:, where][None]
        above = jnp.concatenate([x[:1], x[:-1]], axis=0)
        below = jnp.concatenate([x[1:], x[-1:]], axis=0)
        stepped = x + rate * (above - 2.0 * x + below) - 0.05 * x * x * x
        top = stepped[:1] + surf_ref[:, where][None]
        stepped = jnp.concatenate([top, stepped[1:]], axis=0)
        land = jnp.broadcast_to(land_ref[:, where][None], x.shape) > 0
        fc_ref[me, :, :, where] = jnp.where(land, stepped, x).astype(jnp.bfloat16)
        return carry

    lax.fori_loop(0, columns // lanes, mix, 0)
    pl.semaphore_wait(barrier, n_mem - 1 + 2 * REACH)

    def remote(src, dst, send, recv, where):
        return pltpu.make_async_remote_copy(
            src_ref=src,
            dst_ref=dst,
            send_sem=send,
            recv_sem=recv,
            device_id=where,
            device_id_type=MESH,
        )

    started = []

    def go(copy):
        copy.start()
        started.append(copy)

    def weight_copy(j):
        return remote(
            weight_hbm.at[j],
            near_ref.at[j],
            w_send.at[j],
            w_recv.at[j],
            {"tile": lax.rem(tile + j - REACH + n_tile, n_tile)},
        )

    def fc_copy(q, owner, lane, target):
        block = fc_ref.at[owner, pl.ds(cuts[q], cuts[q + 1] - cuts[q])]
        return remote(block, block, fc_send.at[q, lane], fc_recv.at[q, owner], {"mem": target})

    def seen_copy(h, owner, lane, target):
        block = seen_ref.at[owner, h]
        return remote(
            block, block, seen_send.at[h, lane], seen_recv.at[h, owner], {"mem": target}
        )

    def own_fc(q):
        for index, peer in enumerate(across):
            go(fc_copy(q, me, index, peer))
        go(fc_copy(q, me, n_y - 1, sibling))

    def relay_fc(q):
        for index, peer in enumerate(across):
            fc_copy(q, peer, index, peer).wait_recv()
            go(fc_copy(q, peer, n_y + index, sibling))

    for j in range(near):
        if j != REACH:
            go(weight_copy(j))
    own_fc(0)

    for copy in inputs[3:]:
        copy.wait()
    half = slots // HALVES
    width = min(half, 512)
    for h in range(HALVES):

        def pick(step, carry, h=h):
            inner = pl.ds(pl.multiple_of(step * width, width), width)
            where = pl.ds(pl.multiple_of(h * half + step * width, width), width)
            rows = lax.broadcasted_iota(jnp.int32, (columns, width), 0)
            hot = jnp.where(rows == pos_ref[:, where], 1.0, 0.0).astype(jnp.bfloat16)
            flat = fc_ref[me].reshape(fields * members, columns)
            found = jnp.dot(flat, hot, preferred_element_type=jnp.float32)
            wanted = jnp.broadcast_to(field_ref[:, where], (members, width))
            total = found[:members]
            for f in range(1, fields):
                total = jnp.where(wanted == f, found[f * members : (f + 1) * members], total)
            seen_ref[me, h, :, inner] = total.astype(jnp.bfloat16)
            return carry

        lax.fori_loop(0, half // width, pick, 0)
        for index, peer in enumerate(across):
            go(seen_copy(h, me, index, peer))
        go(seen_copy(h, me, n_y - 1, sibling))

    n_cuts = len(cuts) - 1
    for q in range(1, n_cuts):
        own_fc(q)

    base = valid_ref[...].astype(jnp.float32) / error_ref[...].astype(jnp.float32)
    slot_ref[near] = value_ref[...].astype(jnp.float32)
    for spare in range(near + 1, slot_ref.shape[0]):
        slot_ref[spare] = jnp.zeros_like(base)
    for j in range(near):
        if j != REACH:
            weight_copy(j).wait_recv()
        slot_ref[j] = base * near_ref[j]
    acc_ref[...] = jnp.zeros_like(acc_ref)
    relay_fc(0)

    for h in range(HALVES):
        for index, peer in enumerate(across):
            seen_copy(h, peer, index, peer).wait_recv()
            go(seen_copy(h, peer, n_y + index, sibling))
    for h in range(HALVES):
        for owner in [sibling, *partner_of]:
            seen_copy(h, owner, 0, sibling).wait_recv()

        def gather_stats(step, carry, h=h):
            inner = pl.ds(pl.multiple_of(step * width, width), width)
            seen = jnp.concatenate(
                [seen_ref[m, h, :, inner].astype(jnp.float32) for m in range(n_mem)], axis=0
            )
            average = jnp.mean(seen, axis=0, keepdims=True)
            deviation = seen - average
            first = (h * half + step * width) // lanes
            rinv = jnp.concatenate(
                [slot_ref[:, first + r, :] for r in range(width // lanes)], axis=1
            )
            innovation = rinv[near : near + 1] - average
            high = deviation.astype(jnp.bfloat16)
            low = (deviation - high.astype(jnp.float32)).astype(jnp.bfloat16)
            right = jnp.concatenate([high, low], axis=0)
            pulls = rinv * innovation
            rows = [(deviation * rinv[j : j + 1]).astype(jnp.bfloat16) for j in range(near)]
            rows.append(jnp.concatenate([pulls, jnp.zeros_like(pulls)], axis=0).astype(jnp.bfloat16))
            left = jnp.concatenate(rows, axis=0)
            sums = lax.dot_general(
                left, right, (((1,), (1,)), ((), ())), preferred_element_type=jnp.float32
            )
            acc_ref[...] += sums
            return carry

        lax.fori_loop(0, half // width, gather_stats, 0)

    fold = everyone // 2
    for j in range(near):
        sums = acc_ref[j * everyone : (j + 1) * everyone]
        sums = sums[:, :everyone] + sums[:, everyone:]
        part_ref[j, :fold] = jnp.concatenate([sums[:fold], sums[fold:]], axis=1)
        part_ref[j, fold:] = jnp.broadcast_to(
            acc_ref[near * everyone + j : near * everyone + j + 1], (8, 2 * everyone)
        )

    def part_copy(j):
        return remote(
            part_ref.at[j],
            got_ref.at[j],
            p_send.at[j],
            p_recv.at[j],
            {"tile": lax.rem(tile - (j - REACH) + n_tile, n_tile)},
        )

    for j in range(near):
        if j != REACH:
            go(part_copy(j))
    for q in range(1, n_cuts - 2):
        relay_fc(q)
    summed = part_ref[REACH]
    for j in range(near):
        if j != REACH:
            part_copy(j).wait_recv()
            summed = summed + got_ref[j]
    summed = summed / (everyone - 1.0)
    spread = jnp.concatenate([summed[:fold, :everyone], summed[:fold, everyone:]], axis=0)
    pulled = summed[fold:, :everyone] + summed[fold:, everyone:]
    rows = lax.broadcasted_iota(jnp.int32, (everyone, everyone), 0)
    identity = jnp.where(
        rows == lax.broadcasted_iota(jnp.int32, (everyone, everyone), 1), 1.0, 0.0
    )
    system = identity + spread
    scale = jnp.sqrt(jnp.sum(system * system, keepdims=True))
    current = system / scale
    root = 1.5 * identity - 0.5 * current
    current = exact_dot(current, root)
    for sweep in range(1, NS_ITERS):
        middle = 1.5 * identity - 0.5 * exact_dot(root, current)
        if sweep < NS_ITERS - 1:
            current = exact_dot(current, middle)
        root = exact_dot(middle, root)
    root = root / jnp.sqrt(scale)
    mean_weight = exact_dot(exact_dot(pulled, root), root)[:1]
    turned = root + mean_weight
    turned = turned + (1.0 - jnp.sum(turned, axis=1, keepdims=True)) / everyone
    for m in range(n_mem):
        tsend_ref[m, :, :everyone] = turned[m * members : (m + 1) * members]
        tsend_ref[m, :, everyone:] = jnp.zeros((members, everyone), jnp.float32)

    def t_copy(owner, target, lane):
        return remote(
            tsend_ref.at[target],
            trecv_ref.at[owner],
            t_send.at[lane],
            t_recv.at[owner],
            {"mem": target},
        )

    for step in range(1, n_mem):
        go(t_copy(me, lax.rem(me + step, n_mem), step))
    trecv_ref[me] = tsend_ref[me]
    for q in range(n_cuts - 2, n_cuts):
        relay_fc(q)
    for q in range(n_cuts):
        for owner in [sibling, *partner_of]:
            fc_copy(q, owner, 0, sibling).wait_recv()
    for step in range(1, n_mem):
        t_copy(lax.rem(me + step, n_mem), me, step).wait_recv()

    wide = columns // n_mem
    group = 8

    def apply(block, carry):
        where = pl.ds(pl.multiple_of(block * wide, wide), wide)
        weights = trecv_ref[block][:, :everyone]
        high = weights.astype(jnp.bfloat16)
        low = (weights - high.astype(jnp.float32)).astype(jnp.bfloat16)
        left = jnp.concatenate([high, low], axis=0)
        land = jnp.broadcast_to(land_ref[:, where], (members, wide)) > 0
        for first in range(0, fields, group):
            states = jnp.concatenate(
                [
                    jnp.concatenate([fc_ref[m, f, :, where] for m in range(n_mem)], axis=0)
                    for f in range(first, first + group)
                ],
                axis=1,
            )
            both = jnp.dot(left, states, preferred_element_type=jnp.float32)
            total = both[:members] + both[members:]
            for f in range(group):
                moved_ref[first + f, :, :] = jnp.where(
                    land,
                    total[:, f * wide : (f + 1) * wide],
                    fc_ref[me, first + f, :, where].astype(jnp.float32),
                )
        out_ref[:, :, where] = jnp.transpose(moved_ref[...], (1, 0, 2)).astype(jnp.bfloat16)
        return carry

    lax.fori_loop(0, n_mem, apply, 0)
    for copy in started:
        copy.wait_send()


def on_device(
    n_mem,
    n_tile,
    ensemble_profiles_before,
    mixing_coefficient,
    surface_driver,
    terrain_indicator,
    measured_profile_position,
    measured_field_index,
    obs_valid,
    obs_value,
    obs_error,
    local_weight,
):
    members, fields, columns = ensemble_profiles_before.shape
    slots = measured_field_index.shape[0]
    everyone = members * n_mem
    near = 2 * REACH + 1
    n_y = n_mem // CORES
    cuts = (0, *[int(fields * cut) for cut in FIELD_CUTS], fields)
    n_cuts = len(cuts) - 1
    row = lambda a: a.reshape(1, -1)
    table = lambda a: a.reshape(-1, 128)
    far = pl.BlockSpec(memory_space=pltpu.HBM)
    dma = pltpu.SemaphoreType.DMA
    return pl.pallas_call(
        functools.partial(kernel, n_mem, n_tile, cuts),
        out_shape=pltpu.VMEM(ensemble_profiles_before.shape, jnp.bfloat16),
        in_specs=[far] * 10,
        out_specs=pl.BlockSpec(memory_space=pltpu.VMEM),
        scratch_shapes=[
            pltpu.VMEM((members, fields, columns), jnp.bfloat16),
            pltpu.VMEM((1, columns), jnp.float32),
            pltpu.VMEM((members, columns), jnp.float32),
            pltpu.VMEM((1, columns), jnp.int32),
            pltpu.VMEM((1, slots), jnp.int32),
            pltpu.VMEM((1, slots), jnp.int32),
            pltpu.VMEM((slots // 128, 128), jnp.int32),
            pltpu.VMEM((slots // 128, 128), jnp.bfloat16),
            pltpu.VMEM((slots // 128, 128), jnp.bfloat16),
            pltpu.VMEM((n_mem, fields, members, columns), jnp.bfloat16),
            pltpu.VMEM((n_mem, HALVES, members, slots // HALVES), jnp.bfloat16),
            pltpu.VMEM((near, slots // 128, 128), jnp.float32),
            pltpu.VMEM((8, slots // 128, 128), jnp.float32),
            pltpu.VMEM((near * everyone + 16, 2 * everyone), jnp.float32),
            pltpu.VMEM((near, everyone // 2 + 8, 2 * everyone), jnp.float32),
            pltpu.VMEM((near, everyone // 2 + 8, 2 * everyone), jnp.float32),
            pltpu.VMEM((n_mem, members, 2 * everyone), jnp.float32),
            pltpu.VMEM((n_mem, members, 2 * everyone), jnp.float32),
            pltpu.VMEM((fields, members, columns // n_mem), jnp.float32),
            dma((columns // 128,)),
            dma((9,)),
            dma((HALVES, 2 * n_y)),
            dma((HALVES, n_mem)),
            dma((n_cuts, 2 * n_y)),
            dma((n_cuts, n_mem)),
            dma((near,)),
            dma((near,)),
            dma((near,)),
            dma((near,)),
            dma((n_mem,)),
            dma((n_mem,)),
        ],
        compiler_params=pltpu.CompilerParams(
            collective_id=0, has_side_effects=True, vmem_limit_bytes=66_000_000
        ),
    )(
        ensemble_profiles_before,
        row(mixing_coefficient),
        surface_driver,
        row(terrain_indicator),
        row(measured_profile_position),
        row(measured_field_index),
        table(obs_valid),
        table(obs_value),
        table(obs_error),
        local_weight.reshape(near, slots // 128, 128),
    )


def fits(n_mem, n_tile, ensemble, slots):
    members, fields, columns = ensemble[0] // n_mem, ensemble[1], ensemble[2] // n_tile
    return (
        n_mem % CORES == 0
        and n_tile > 2 * REACH
        and members % 16 == 0
        and fields % 8 == 0
        and columns % (128 * n_mem) == 0
        and slots // n_tile % (512 * HALVES) == 0
    )


def solution(mesh):
    in_specs = (
        P("mem", None, "tile"),
        P("tile"),
        P("mem", "tile"),
        P("tile"),
        P("tile"),
        P("tile"),
        P("tile"),
        P("tile"),
        P("tile"),
        P("mem", "tile", None),
    )
    out_specs = P("mem", None, "tile")

    def run(*args):
        sizes = mesh.shape["mem"], mesh.shape["tile"]
        body = plain_on_device
        if fits(*sizes, args[0].shape, args[5].shape[0]):
            body = functools.partial(on_device, *sizes)
        return jax.shard_map(
            body, mesh=mesh, in_specs=in_specs, out_specs=out_specs, check_vma=False
        )(*args)

    return run
```

profile of v0, /device:TPU:1, one launch (start us, length us, event | category | flops | bytes accessed | tf_op | source)
XLA Modules:
  0.0 28.6 jit_solution(10165739218721971493)
XLA Ops:
  0.0 27.7 %shard_map.100 = bf16[16,40,512]{2,1,0:T(8,128)(2,1)S(1)} custom-call(bf16[16,40,512]{2,1,0:T(8,128)(2,1)} %ens_hbm.1, f32[1,512]{1,0:T(1,128)} %bitcast.14, f32[16,512]{1,0:T(8,128)} %surf_hbm.1, s32[1,512]{1,0:T(1,128)} %bitcast.15, s32[1,4096]{1,0:T(1,128)} %bitcast.9, s32[1,4096]{1,0:T(1,128)} %bitcast.10, s32[32,128]{1,0:T(8,128)} %bitcast.11, ...), custom_call_target="tpu_custom_call" | custom-call | tf_op jit(solution)/shard_map/pallas_call | solution.py:534
  27.7 0.8 %copy.12 = bf16[16,40,512]{2,1,0:T(8,128)(2,1)} copy(bf16[16,40,512]{2,1,0:T(8,128)(2,1)S(1)} %shard_map.100) | data formatting | bytes 1310720
where the time goes:
time: 28.7 us; the launch traced here: 28.6 us
  Pallas kernels  27.7 us (97%)
  local copies, waits for them, and re-layouts  0.84 us (3%)
    pallas_call x1, Pallas kernels, on_device(): pl.pallas_call(functools.partial(kernel, n_mem, n_tile, cuts), out_shape=...  27.7 us
    unnamed x1, local copies, waits for them, and re-layouts  0.84 us

commit v1 on v0

v1 whole, which is shorter than its diff:
```python
import functools

import jax
import jax.numpy as jnp
from jax import lax
from jax.experimental import pallas as pl
from jax.experimental.pallas import tpu as pltpu
from jax.sharding import PartitionSpec as P

REACH = 2
NS_ITERS = 3


EXACT = lax.Precision.HIGHEST


def from_behind(value, axis, steps):
    count = lax.axis_size(axis)
    pairs = [(source, (source + steps) % count) for source in range(count)]
    return lax.ppermute(value, axis, pairs)


def vertical_mixing_step(
    ensemble_profiles_before, mixing_coefficient, surface_driver, terrain_indicator
):
    values = ensemble_profiles_before.astype(jnp.float32)
    above_layer = jnp.concatenate([values[:, :1], values[:, :-1]], axis=1)
    below_layer = jnp.concatenate([values[:, 1:], values[:, -1:]], axis=1)
    diffused = values + mixing_coefficient[None, None, :] * (
        above_layer - 2.0 * values + below_layer
    )
    stepped = diffused - 0.05 * values * values * values
    surface = jnp.concatenate([stepped[:, :1] + surface_driver[:, None, :], stepped[:, 1:]], axis=1)
    result = jnp.where(terrain_indicator[None, None, :] > 0, surface, values)
    return result.astype(jnp.bfloat16)


def measurement_operator(background_ensemble, measured_profile_position, measured_field_index):
    profile_sequence = background_ensemble.shape[2]
    unrolled_ensemble = background_ensemble.reshape(background_ensemble.shape[0], -1)
    slot_index = measured_field_index * profile_sequence + measured_profile_position
    return jnp.take(unrolled_ensemble, slot_index, axis=1)


def prepare(window):
    ensemble_profiles = window.shape[0] - 3
    measured_quantities = window[:ensemble_profiles].astype(jnp.float32)
    average = jnp.mean(measured_quantities, axis=0)
    deviation = measured_quantities - average
    innovation = window[ensemble_profiles].astype(jnp.float32) - average
    obs_precision = window[ensemble_profiles + 2].astype(jnp.float32) / window[
        ensemble_profiles + 1
    ].astype(jnp.float32)
    return (deviation, innovation, obs_precision)


def weights_for(deviation, innovation, precision, portions):
    ensemble_profiles = deviation.shape[0]
    portion_width = deviation.shape[1] // portions
    spread = jnp.zeros((ensemble_profiles, ensemble_profiles), jnp.float32)
    for portion_index in range(portions):
        portion = deviation[:, portion_index * portion_width : (portion_index + 1) * portion_width]
        scaled = (
            portion
            * precision[None, portion_index * portion_width : (portion_index + 1) * portion_width]
        )
        spread = spread + jnp.dot(
            scaled, portion.T, precision=EXACT, preferred_element_type=jnp.float32
        )
    spread = spread / (ensemble_profiles - 1.0)
    pulled = jnp.dot(
        deviation, precision * innovation, precision=EXACT, preferred_element_type=jnp.float32
    ) / (ensemble_profiles - 1.0)
    identity = jnp.eye(ensemble_profiles, dtype=jnp.float32)
    system = identity + spread
    norm_scale = jnp.sqrt(jnp.sum(system * system))

    def newton(sweep, carry):
        current, inv_root = carry
        middle = 1.5 * identity - 0.5 * jnp.dot(inv_root, current, precision=EXACT)
        return (
            jnp.dot(current, middle, precision=EXACT),
            jnp.dot(middle, inv_root, precision=EXACT),
        )

    current, inv_root = lax.fori_loop(0, NS_ITERS, newton, (system / norm_scale, identity))
    inv_root = inv_root / jnp.sqrt(norm_scale)
    inverse = jnp.dot(inv_root, inv_root, precision=EXACT)
    mean_weight = jnp.dot(inverse, pulled, precision=EXACT)
    return inv_root + mean_weight[:, None]


def update(states, transform, land_block):
    values = states.astype(jnp.float32)
    average = jnp.mean(values, axis=0)
    deviation = values - average[None]
    moved = jnp.einsum("isc,ij->jsc", deviation, transform, precision=EXACT)
    result = jnp.where(land_block[None, None, :] > 0, average[None] + moved, values)
    return result.astype(jnp.bfloat16)


def plain_on_device(
    ensemble_profiles_before,
    mixing_coefficient,
    surface_driver,
    terrain_indicator,
    measured_profile_position,
    measured_field_index,
    obs_valid,
    obs_value,
    obs_error,
    local_weight,
):
    background_ensemble = vertical_mixing_step(
        ensemble_profiles_before, mixing_coefficient, surface_driver, terrain_indicator
    )
    measured_quantities = measurement_operator(
        background_ensemble, measured_profile_position, measured_field_index
    )
    metadata = jnp.stack([obs_value, obs_error, obs_valid.astype(jnp.bfloat16)])
    own_rows = jnp.concatenate([measured_quantities, metadata], axis=0)
    pieces = []
    for offset in range(-REACH, REACH + 1):
        if offset == 0:
            pieces.append(own_rows)
        else:
            pieces.append(from_behind(own_rows, "tile", -offset))
    nearby = jnp.concatenate(pieces, axis=1)
    members_here = measured_quantities.shape[0]
    everyone = lax.all_gather(nearby[:members_here], "mem", axis=0, tiled=True)
    window = jnp.concatenate([everyone, nearby[members_here:]], axis=0)
    regrouped_states = lax.all_to_all(
        background_ensemble, "mem", split_axis=2, concat_axis=0, tiled=True
    )
    deviation, innovation, obs_precision = prepare(window)
    columns_here = regrouped_states.shape[2]
    local_land = lax.dynamic_slice_in_dim(
        terrain_indicator, lax.axis_index("mem") * columns_here, columns_here
    )
    transform = weights_for(
        deviation, innovation, obs_precision * local_weight[0, 0], 2 * REACH + 1
    )
    outputs = update(regrouped_states, transform, local_land)
    return lax.all_to_all(outputs, "mem", split_axis=0, concat_axis=2, tiled=True)


MESH = pl.DeviceIdType.MESH
CHUNKS = 4
CORES = 2
GATE = CORES - 1


def rounded_dot(a, b):
    return jnp.dot(a, b, preferred_element_type=jnp.float32)


def halves(a):
    high = a.astype(jnp.bfloat16)
    return high, (a - high.astype(jnp.float32)).astype(jnp.bfloat16)


def fine_dot(a, b):
    (a_high, a_low), (b_high, b_low) = a, b
    return rounded_dot(a_high, b_high) + (rounded_dot(a_high, b_low) + rounded_dot(a_low, b_high))


def drain(ref, sem):
    pltpu.make_async_copy(ref, ref, sem).wait()


def kernel(
    n_mem,
    n_tile,
    pieces,
    ens_hbm,
    mix_hbm,
    surf_hbm,
    land_hbm,
    pos_hbm,
    field_hbm,
    valid_hbm,
    value_hbm,
    error_hbm,
    weight_hbm,
    out_ref,
    ens_ref,
    mix_ref,
    surf_ref,
    land_ref,
    pos_ref,
    field_ref,
    valid_ref,
    value_ref,
    error_ref,
    fc_ref,
    seen_ref,
    near_ref,
    slot_ref,
    acc_ref,
    part_ref,
    got_ref,
    tsend_ref,
    trecv_ref,
    moved_ref,
    ens_sem,
    in_sem,
    seen_send,
    seen_across,
    seen_all,
    fc_send,
    fc_across,
    fc_block,
    tile_send,
    tile_recv,
    t_send,
    t_recv,
    hello,
    ready,
):
    members, fields, columns = ens_ref.shape
    everyone = members * n_mem
    slots = pos_ref.shape[1]
    near = 2 * REACH + 1
    wide = columns // n_mem
    me, tile = lax.axis_index("mem"), lax.axis_index("tile")
    n_y = n_mem // CORES
    y, core = me // CORES, lax.rem(me, CORES)
    sibling = y * CORES + (1 - core)
    across = [lax.rem(y + step, n_y) * CORES + core for step in range(1, n_y)]
    gate = me == GATE

    barrier = pltpu.get_barrier_semaphore()
    for step in range(1, n_mem):
        peer = lax.rem(me + step, n_mem)

        @pl.when(peer != GATE)
        def _(peer=peer):
            pl.semaphore_signal(barrier, inc=1, device_id={"mem": peer}, device_id_type=MESH)

    def ens_copy(step):
        where = pl.ds(pl.multiple_of(step * wide, wide), wide)
        return pltpu.make_async_copy(
            ens_hbm.at[:, :, where], ens_ref.at[:, :, where], ens_sem.at[step]
        )

    groups = [
        [(mix_hbm, mix_ref), (surf_hbm, surf_ref), (land_hbm, land_ref)],
        [(pos_hbm, pos_ref), (field_hbm, field_ref)],
        [
            (valid_hbm, valid_ref),
            (value_hbm, value_ref),
            (error_hbm, error_ref),
            (weight_hbm.at[REACH], near_ref.at[REACH]),
        ],
    ]
    loads = [
        [pltpu.make_async_copy(src, dst, in_sem.at[g]) for src, dst in group]
        for g, group in enumerate(groups)
    ]
    for copy in loads[0]:
        copy.start()
    for step in range(n_mem):
        ens_copy(step).start()
    for group in loads[1:]:
        for copy in group:
            copy.start()

    def remote(src, dst, send, recv, where):
        return pltpu.make_async_remote_copy(
            src_ref=src,
            dst_ref=dst,
            send_sem=send,
            recv_sem=recv,
            device_id=where,
            device_id_type=MESH,
        )

    def fc_copy(piece, owner, recv, target):
        block, first, last = pieces[piece]
        ref = fc_ref.at[owner, block, pl.ds(first, last - first)]
        return remote(ref, ref, fc_send.at[0], recv, {"mem": target})

    def fc_over(piece, owner, index, target):
        return fc_copy(piece, owner, fc_across.at[piece, index], target)

    def fc_near(piece, owner):
        return fc_copy(piece, owner, fc_block.at[pieces[piece][0]], sibling)

    def own_fc(piece):
        for index, peer in enumerate(across):
            fc_over(piece, me, n_y - 2 - index, peer).start()
        fc_near(piece, me).start()

    def relay_fc(piece):
        for index, peer in enumerate(across):
            fc_over(piece, peer, index, peer).wait_recv()
            fc_near(piece, peer).start()

    def seen_copy(h, owner, recv, target):
        ref = seen_ref.at[owner, h]
        return remote(ref, ref, seen_send.at[0], recv, {"mem": target})

    def own_seen(h):
        for index, peer in enumerate(across):
            seen_copy(h, me, seen_across.at[h, n_y - 2 - index], peer).start()
        seen_copy(h, me, seen_all.at[h], sibling).start()

    def relay_seen(h):
        for index, peer in enumerate(across):
            seen_copy(h, peer, seen_across.at[h, index], peer).wait_recv()
            seen_copy(h, peer, seen_all.at[h], sibling).start()

    def tile_peer(offset):
        return {"tile": lax.rem(tile + offset + n_tile, n_tile)}

    def mix_block(step):
        where = pl.ds(pl.multiple_of(step * wide, wide), wide)
        ens_copy(step).wait()
        x = jnp.transpose(ens_ref[:, :, where].astype(jnp.float32), (1, 0, 2))
        rate = mix_ref[:, where][None]
        above = jnp.concatenate([x[:1], x[:-1]], axis=0)
        below = jnp.concatenate([x[1:], x[-1:]], axis=0)
        stepped = x + rate * (above - 2.0 * x + below) - 0.05 * x * x * x
        top = stepped[:1] + surf_ref[:, where][None]
        stepped = jnp.concatenate([top, stepped[1:]], axis=0)
        land = jnp.broadcast_to(land_ref[:, where][None], x.shape) > 0
        fc_ref[me, step] = jnp.where(land, stepped, x).astype(jnp.bfloat16)

    head_bytes = 4 * columns * (members + 2)
    drain(acc_ref.at[pl.ds(0, head_bytes // 512)], in_sem.at[0])
    mix_block(0)

    @pl.when(jnp.logical_not(gate))
    def _():
        pl.semaphore_wait(barrier, n_mem - 1)
        pl.semaphore_signal(hello, inc=1, device_id={"mem": GATE}, device_id_type=MESH)
        own_fc(0)

    def mix(step, carry):
        mix_block(step)
        return carry

    lax.fori_loop(1, n_mem, mix, 0)

    @pl.when(gate)
    def _():
        pl.semaphore_wait(hello, n_mem - 1)
        for offset in range(-REACH, REACH + 1):
            if offset:
                pl.semaphore_signal(
                    barrier, inc=1, device_id=tile_peer(offset), device_id_type=MESH
                )
        own_fc(0)

    drain(slot_ref.at[pl.ds(0, 2)], in_sem.at[1])
    share = slots // CHUNKS
    width = min(share, 512)
    flat = jnp.concatenate(
        [fc_ref[me, b].reshape(fields * members, wide) for b in range(n_mem)], axis=1
    )
    for h in range(CHUNKS):
        for step in range(share // width):
            where = pl.ds(h * share + step * width, width)
            rows = lax.broadcasted_iota(jnp.int32, (columns, width), 0)
            hot = jnp.where(rows == pos_ref[:, where], 1.0, 0.0).astype(jnp.bfloat16)
            found = rounded_dot(flat, hot)
            wanted = jnp.broadcast_to(field_ref[:, where], (members, width))
            total = found[:members]
            for f in range(1, fields):
                total = jnp.where(wanted == f, found[f * members : (f + 1) * members], total)
            seen_ref[me, h, :, pl.ds(step * width, width)] = total.astype(jnp.bfloat16)
        own_seen(h)

    n_pieces = len(pieces)
    for piece in range(1, n_pieces):
        own_fc(piece)

    @pl.when(gate)
    def _():
        pl.semaphore_wait(barrier, 2 * REACH)
        for step in range(1, n_mem):
            pl.semaphore_signal(
                ready, inc=1, device_id={"mem": lax.rem(me + step, n_mem)}, device_id_type=MESH
            )

    @pl.when(jnp.logical_not(gate))
    def _():
        pl.semaphore_wait(ready, 1)

    for j in range(near):
        if j != REACH:
            remote(
                weight_hbm.at[j],
                near_ref.at[j],
                tile_send.at[0],
                tile_recv.at[0],
                tile_peer(j - REACH),
            ).start()
    drain(slot_ref.at[pl.ds(0, 3)], in_sem.at[2])
    base = valid_ref[...].astype(jnp.float32) / error_ref[...].astype(jnp.float32)
    slot_ref[near] = value_ref[...].astype(jnp.float32)
    for spare in range(near + 1, slot_ref.shape[0]):
        slot_ref[spare] = jnp.zeros_like(base)
    slot_ref[REACH] = base * near_ref[REACH]
    acc_ref[...] = jnp.zeros_like(acc_ref)

    relay_fc(0)
    lanes = 128

    relay_seen(0)
    relay_seen(1)

    drain(near_ref.at[pl.ds(0, near - 1)], tile_recv.at[0])
    for j in range(near):
        if j != REACH:
            slot_ref[j] = base * near_ref[j]

    for h in range(CHUNKS):
        if h >= 1 and h + 1 < CHUNKS:
            relay_seen(h + 1)
        drain(seen_ref.at[pl.ds(0, n_y), h], seen_all.at[h])

        def gather_stats(step, carry, h=h):
            inner = pl.ds(pl.multiple_of(step * width, width), width)
            seen = jnp.concatenate(
                [seen_ref[m, h, :, inner].astype(jnp.float32) for m in range(n_mem)], axis=0
            )
            average = jnp.mean(seen, axis=0, keepdims=True)
            deviation = seen - average
            first = (h * share + step * width) // lanes
            rinv = jnp.concatenate(
                [slot_ref[:, first + r, :] for r in range(width // lanes)], axis=1
            )
            innovation = rinv[near : near + 1] - average
            pulls = rinv * innovation
            rows = [(deviation * rinv[j : j + 1]).astype(jnp.bfloat16) for j in range(near)]
            rows.append(jnp.concatenate([pulls, jnp.zeros_like(pulls)], axis=0).astype(jnp.bfloat16))
            sums = lax.dot_general(
                jnp.concatenate(rows, axis=0),
                deviation.astype(jnp.bfloat16),
                (((1,), (1,)), ((), ())),
                preferred_element_type=jnp.float32,
            )
            acc_ref[:, :everyone] += sums
            return carry

        lax.fori_loop(0, share // width, gather_stats, 0)

    fold = everyone // 2
    for j in range(near):
        sums = acc_ref[j * everyone : (j + 1) * everyone, :everyone]
        part_ref[j, :fold] = jnp.concatenate([sums[:fold], sums[fold:]], axis=1)
        part_ref[j, fold:] = jnp.broadcast_to(
            acc_ref[near * everyone + j : near * everyone + j + 1], (8, 2 * everyone)
        )

    for j in range(near):
        if j != REACH:
            remote(
                part_ref.at[j],
                got_ref.at[j],
                tile_send.at[1],
                tile_recv.at[1],
                tile_peer(REACH - j),
            ).start()

    relay_fc(1)
    relay_fc(2)

    summed = part_ref[REACH]
    drain(got_ref.at[pl.ds(0, near - 1)], tile_recv.at[1])

    for j in range(near):
        if j != REACH:
            summed = summed + got_ref[j]
    summed = summed / (everyone - 1.0)
    spread = jnp.concatenate([summed[:fold, :everyone], summed[:fold, everyone:]], axis=0)
    pulled = summed[fold:, :everyone]
    rows = lax.broadcasted_iota(jnp.int32, (everyone, everyone), 0)
    identity = jnp.where(
        rows == lax.broadcasted_iota(jnp.int32, (everyone, everyone), 1), 1.0, 0.0
    )
    system = identity + spread
    square = jnp.sum(system * system, keepdims=True)
    scale = jnp.sqrt(square)
    parts = halves(system)
    second = fine_dot(parts, parts) / square
    current = system / scale
    parts, second_parts = halves(current), halves(second)
    third = fine_dot(second_parts, parts)
    fourth = fine_dot(second_parts, second_parts)
    root = 2.25 * identity - 2.4375 * current + 1.6875 * second - 0.5625 * third + 0.0625 * fourth
    root_parts = halves(root)
    inner_parts = halves(fine_dot(parts, root_parts))
    outer_parts = halves(fine_dot(root_parts, root_parts))
    root = 1.5 * root - 0.5 * fine_dot(inner_parts, outer_parts)
    root_parts = halves(root)
    ones = jnp.ones((everyone, everyone), jnp.bfloat16)
    sums = rounded_dot(root_parts[0], ones) + rounded_dot(root_parts[1], ones)
    drawn = halves(fine_dot(halves(pulled), root_parts))
    mean_weight = fine_dot(drawn, root_parts)[:1] / scale
    weight_sum = fine_dot(drawn, halves(sums))[:1] / scale
    turned = root / jnp.sqrt(scale) + mean_weight
    turned = turned + (1.0 - sums / jnp.sqrt(scale) - weight_sum) / everyone
    for m in range(n_mem):
        tsend_ref[m, :, :everyone] = turned[m * members : (m + 1) * members]
        tsend_ref[m, :, everyone:] = jnp.zeros((members, everyone), jnp.float32)

    for step in range(1, n_mem):
        target = lax.rem(me + step, n_mem)
        remote(
            tsend_ref.at[target],
            trecv_ref.at[me],
            t_send.at[0],
            t_recv.at[0],
            {"mem": target},
        ).start()
    trecv_ref[me] = tsend_ref[me]

    group = 8

    def apply(block):
        where = pl.ds(block * wide, wide)
        left = jnp.concatenate(halves(trecv_ref[block][:, :everyone]), axis=0)
        land = jnp.broadcast_to(land_ref[:, where], (members, wide)) > 0
        for first in range(0, fields, group):
            states = jnp.concatenate(
                [
                    jnp.concatenate([fc_ref[m, block, f] for m in range(n_mem)], axis=0)
                    for f in range(first, first + group)
                ],
                axis=1,
            )
            both = rounded_dot(left, states)
            total = both[:members] + both[members:]
            for f in range(group):
                moved_ref[first + f, :, :] = jnp.where(
                    land,
                    total[:, f * wide : (f + 1) * wide],
                    fc_ref[me, block, first + f].astype(jnp.float32),
                )
        out_ref[:, :, where] = jnp.transpose(moved_ref[...], (1, 0, 2)).astype(jnp.bfloat16)

    for piece in range(3, n_pieces - 1):
        relay_fc(piece)

    drain(trecv_ref.at[pl.ds(0, n_mem - 1)], t_recv.at[0])

    for block in range(n_mem):
        if block == n_mem - 2:
            relay_fc(n_pieces - 1)
        drain(fc_ref.at[pl.ds(0, n_y), block], fc_block.at[block])
        apply(block)

    drain(fc_ref.at[pl.ds(0, n_mem - 1)], fc_send.at[0])
    drain(seen_ref.at[pl.ds(0, n_mem - 1)], seen_send.at[0])
    drain(near_ref.at[pl.ds(0, near - 1)], tile_send.at[0])
    drain(part_ref.at[pl.ds(0, near - 1)], tile_send.at[1])
    drain(tsend_ref.at[pl.ds(0, n_mem - 1)], t_send.at[0])


def on_device(
    n_mem,
    n_tile,
    ensemble_profiles_before,
    mixing_coefficient,
    surface_driver,
    terrain_indicator,
    measured_profile_position,
    measured_field_index,
    obs_valid,
    obs_value,
    obs_error,
    local_weight,
):
    members, fields, columns = ensemble_profiles_before.shape
    slots = measured_field_index.shape[0]
    everyone = members * n_mem
    near = 2 * REACH + 1
    n_y = n_mem // CORES
    wide = columns // n_mem
    half = fields // 2
    pieces = [(0, 0, half), (0, half, fields)]
    pieces += [(block, 0, fields) for block in range(1, n_mem - 1)]
    pieces += [(n_mem - 1, 0, half), (n_mem - 1, half, fields)]
    row = lambda a: a.reshape(1, -1)
    table = lambda a: a.reshape(-1, 128)
    far = pl.BlockSpec(memory_space=pltpu.HBM)
    dma = pltpu.SemaphoreType.DMA
    return pl.pallas_call(
        functools.partial(kernel, n_mem, n_tile, pieces),
        out_shape=pltpu.VMEM(ensemble_profiles_before.shape, jnp.bfloat16),
        in_specs=[far] * 10,
        out_specs=pl.BlockSpec(memory_space=pltpu.VMEM),
        scratch_shapes=[
            pltpu.VMEM((members, fields, columns), jnp.bfloat16),
            pltpu.VMEM((1, columns), jnp.float32),
            pltpu.VMEM((members, columns), jnp.float32),
            pltpu.VMEM((1, columns), jnp.int32),
            pltpu.VMEM((1, slots), jnp.int32),
            pltpu.VMEM((1, slots), jnp.int32),
            pltpu.VMEM((slots // 128, 128), jnp.int32),
            pltpu.VMEM((slots // 128, 128), jnp.bfloat16),
            pltpu.VMEM((slots // 128, 128), jnp.bfloat16),
            pltpu.VMEM((n_mem, n_mem, fields, members, wide), jnp.bfloat16),
            pltpu.VMEM((n_mem, CHUNKS, members, slots // CHUNKS), jnp.bfloat16),
            pltpu.VMEM((near, slots // 128, 128), jnp.float32),
            pltpu.VMEM((8, slots // 128, 128), jnp.float32),
            pltpu.VMEM((near * everyone + 16, 2 * everyone), jnp.float32),
            pltpu.VMEM((near, everyone // 2 + 8, 2 * everyone), jnp.float32),
            pltpu.VMEM((near, everyone // 2 + 8, 2 * everyone), jnp.float32),
            pltpu.VMEM((n_mem, members, 2 * everyone), jnp.float32),
            pltpu.VMEM((n_mem, members, 2 * everyone), jnp.float32),
            pltpu.VMEM((fields, members, wide), jnp.float32),
            dma((n_mem,)),
            dma((3,)),
            dma((1,)),
            dma((CHUNKS, n_y - 1)),
            dma((CHUNKS,)),
            dma((1,)),
            dma((len(pieces), n_y - 1)),
            dma((n_mem,)),
            dma((2,)),
            dma((2,)),
            dma((1,)),
            dma((1,)),
            pltpu.SemaphoreType.REGULAR,
            pltpu.SemaphoreType.REGULAR,
        ],
        compiler_params=pltpu.CompilerParams(
            collective_id=0, has_side_effects=True, vmem_limit_bytes=66_000_000
        ),
    )(
        ensemble_profiles_before,
        row(mixing_coefficient),
        surface_driver,
        row(terrain_indicator),
        row(measured_profile_position),
        row(measured_field_index),
        table(obs_valid),
        table(obs_value),
        table(obs_error),
        local_weight.reshape(near, slots // 128, 128),
    )


def fits(n_mem, n_tile, ensemble, slots):
    members, fields, columns = ensemble[0] // n_mem, ensemble[1], ensemble[2] // n_tile
    return (
        n_mem % CORES == 0
        and n_mem > CORES
        and 2 * members * n_mem == 128
        and n_tile > 2 * REACH
        and members % 16 == 0
        and fields % 8 == 0
        and columns % (128 * n_mem) == 0
        and slots // n_tile % (512 * CHUNKS) == 0
    )


def solution(mesh):
    in_specs = (
        P("mem", None, "tile"),
        P("tile"),
        P("mem", "tile"),
        P("tile"),
        P("tile"),
        P("tile"),
        P("tile"),
        P("tile"),
        P("tile"),
        P("mem", "tile", None),
    )
    out_specs = P("mem", None, "tile")

    def run(*args):
        sizes = mesh.shape["mem"], mesh.shape["tile"]
        body = plain_on_device
        if fits(*sizes, args[0].shape, args[5].shape[0]):
            body = functools.partial(on_device, *sizes)
        return jax.shard_map(
            body, mesh=mesh, in_specs=in_specs, out_specs=out_specs, check_vma=False
        )(*args)

    return run
```

time: 28.7 us -> 27.3 us (0.951)
  the two profiles are of different devices: /device:TPU:1 before, /device:TPU:0 now
where the time goes in v1:
time: 27.3 us; the launch traced here: 27.1 us
  Pallas kernels  26.3 us (96%)
  local copies, waits for them, and re-layouts  0.84 us (3%)
    pallas_call x1, Pallas kernels, on_device(): pl.pallas_call(functools.partial(kernel, n_mem, n_tile, pieces), out_shap...  26.3 us
    unnamed x1, local copies, waits for them, and re-layouts  0.84 us

profile of v1, /device:TPU:0, one launch (start us, length us, event | category | flops | bytes accessed | tf_op | source)
XLA Modules:
  0.0 27.1 jit_solution(5077872993639004046)
XLA Ops:
  0.0 26.3 %shard_map.100 = bf16[16,40,512]{2,1,0:T(8,128)(2,1)S(1)} custom-call(bf16[16,40,512]{2,1,0:T(8,128)(2,1)} %ens_hbm.1, f32[1,512]{1,0:T(1,128)} %bitcast.14, f32[16,512]{1,0:T(8,128)} %surf_hbm.1, s32[1,512]{1,0:T(1,128)} %bitcast.15, s32[1,4096]{1,0:T(1,128)} %bitcast.9, s32[1,4096]{1,0:T(1,128)} %bitcast.10, s32[32,128]{1,0:T(8,128)} %bitcast.11, ...), custom_call_target="tpu_custom_call" | custom-call | tf_op jit(solution)/shard_map/pallas_call | solution.py:590
  26.3 0.8 %copy.12 = bf16[16,40,512]{2,1,0:T(8,128)(2,1)} copy(bf16[16,40,512]{2,1,0:T(8,128)(2,1)S(1)} %shard_map.100) | data formatting | bytes 1310720

commit v2 on v1

--- a/solution.py
+++ b/solution.py
@@ -147,7 +147,7 @@
 MESH = pl.DeviceIdType.MESH
 CHUNKS = 4
 CORES = 2
-GATE = CORES - 1
+GATE = 0
 
 
 def rounded_dot(a, b):
@@ -172,6 +172,7 @@
     n_mem,
     n_tile,
     pieces,
+    units,
     ens_hbm,
     mix_hbm,
     surf_hbm,
@@ -194,6 +195,7 @@
     error_ref,
     fc_ref,
     seen_ref,
+    stage_ref,
     near_ref,
     slot_ref,
     acc_ref,
@@ -205,11 +207,10 @@
     ens_sem,
     in_sem,
     seen_send,
-    seen_across,
-    seen_all,
+    seen_recv,
     fc_send,
     fc_across,
-    fc_block,
+    fc_unit,
     tile_send,
     tile_recv,
     t_send,
@@ -228,14 +229,31 @@
     sibling = y * CORES + (1 - core)
     across = [lax.rem(y + step, n_y) * CORES + core for step in range(1, n_y)]
     gate = me == GATE
+    wraps = tile < REACH
+
+    def both(first, second):
+        return jnp.logical_and(first, second)
 
     barrier = pltpu.get_barrier_semaphore()
     for step in range(1, n_mem):
         peer = lax.rem(me + step, n_mem)
 
-        @pl.when(peer != GATE)
+        @pl.when(jnp.logical_not(both(wraps, peer == GATE)))
         def _(peer=peer):
             pl.semaphore_signal(barrier, inc=1, device_id={"mem": peer}, device_id_type=MESH)
+
+    for offset in range(-REACH, REACH + 1):
+        if offset:
+            there = lax.rem(tile + offset + n_tile, n_tile)
+            for user in range(CORES):
+                who = y * CORES + user
+
+                @pl.when(jnp.logical_or(there >= REACH, user == 0))
+                def _(there=there, who=who):
+                    target = jnp.where(there < REACH, GATE, who)
+                    pl.semaphore_signal(
+                        barrier, inc=1, device_id={"mem": target, "tile": there}, device_id_type=MESH
+                    )
 
     def ens_copy(step):
         where = pl.ds(pl.multiple_of(step * wide, wide), wide)
@@ -250,16 +268,17 @@
             (valid_hbm, valid_ref),
             (value_hbm, value_ref),
             (error_hbm, error_ref),
-            (weight_hbm.at[REACH], near_ref.at[REACH]),
+            (weight_hbm, stage_ref),
         ],
     ]
     loads = [
         [pltpu.make_async_copy(src, dst, in_sem.at[g]) for src, dst in group]
         for g, group in enumerate(groups)
     ]
+    ens_copy(0).start()
     for copy in loads[0]:
         copy.start()
-    for step in range(n_mem):
+    for step in range(1, n_mem):
         ens_copy(step).start()
     for group in loads[1:]:
         for copy in group:
@@ -276,15 +295,20 @@
         )
 
     def fc_copy(piece, owner, recv, target):
-        block, first, last = pieces[piece]
-        ref = fc_ref.at[owner, block, pl.ds(first, last - first)]
+        block, first, stop = pieces[piece][:3]
+        ref = fc_ref.at[owner, block, pl.ds(first, stop - first)]
         return remote(ref, ref, fc_send.at[0], recv, {"mem": target})
 
     def fc_over(piece, owner, index, target):
         return fc_copy(piece, owner, fc_across.at[piece, index], target)
 
     def fc_near(piece, owner):
-        return fc_copy(piece, owner, fc_block.at[pieces[piece][0]], sibling)
+        return fc_copy(piece, owner, fc_unit.at[pieces[piece][3]], sibling)
+
+    def finish_fc(piece):
+        for step in range(1, n_mem):
+            unit = fc_unit.at[pieces[piece][3]]
+            fc_copy(piece, me, unit, lax.rem(me + step, n_mem)).start()
 
     def own_fc(piece):
         for index, peer in enumerate(across):
@@ -296,63 +320,104 @@
             fc_over(piece, peer, index, peer).wait_recv()
             fc_near(piece, peer).start()
 
-    def seen_copy(h, owner, recv, target):
-        ref = seen_ref.at[owner, h]
-        return remote(ref, ref, seen_send.at[0], recv, {"mem": target})
+    def seen_copy(h, send, target):
+        ref = seen_ref.at[me, h]
+        return remote(ref, ref, seen_send.at[send], seen_recv.at[h // CORES], {"mem": target})
 
     def own_seen(h):
-        for index, peer in enumerate(across):
-            seen_copy(h, me, seen_across.at[h, n_y - 2 - index], peer).start()
-        seen_copy(h, me, seen_all.at[h], sibling).start()
-
-    def relay_seen(h):
-        for index, peer in enumerate(across):
-            seen_copy(h, peer, seen_across.at[h, index], peer).wait_recv()
-            seen_copy(h, peer, seen_all.at[h], sibling).start()
+        user = h % CORES
+        for step in range(1, n_y):
+            seen_copy(h, 0, lax.rem(y + step, n_y) * CORES + user).start()
+
+        @pl.when(core != user)
+        def _():
+            seen_copy(h, 1, sibling).start()
 
     def tile_peer(offset):
         return {"tile": lax.rem(tile + offset + n_tile, n_tile)}
 
-    def mix_block(step):
+    def mix_part(step, start, stop):
         where = pl.ds(pl.multiple_of(step * wide, wide), wide)
-        ens_copy(step).wait()
-        x = jnp.transpose(ens_ref[:, :, where].astype(jnp.float32), (1, 0, 2))
+        low, high = max(start - 8, 0), min(stop + 8, fields)
+        x = jnp.transpose(ens_ref[:, low:high, where].astype(jnp.float32), (1, 0, 2))
         rate = mix_ref[:, where][None]
         above = jnp.concatenate([x[:1], x[:-1]], axis=0)
         below = jnp.concatenate([x[1:], x[-1:]], axis=0)
+        keep = slice(start - low, stop - low)
+        x, above, below = x[keep], above[keep], below[keep]
         stepped = x + rate * (above - 2.0 * x + below) - 0.05 * x * x * x
-        top = stepped[:1] + surf_ref[:, where][None]
-        stepped = jnp.concatenate([top, stepped[1:]], axis=0)
+        if start == 0:
+            top = stepped[:1] + surf_ref[:, where][None]
+            stepped = jnp.concatenate([top, stepped[1:]], axis=0)
         land = jnp.broadcast_to(land_ref[:, where][None], x.shape) > 0
-        fc_ref[me, step] = jnp.where(land, stepped, x).astype(jnp.bfloat16)
-
+        fc_ref[me, step, start:stop] = jnp.where(land, stepped, x).astype(jnp.bfloat16)
+
+    def enter():
+        pl.semaphore_wait(barrier, n_mem - 1)
+        pl.semaphore_signal(hello, inc=1, device_id={"mem": GATE}, device_id_type=MESH)
+
+    def send_weights():
+        for j in range(near):
+            for user in range(CORES):
+                if j != REACH:
+                    remote(
+                        stage_ref.at[j, :, user],
+                        near_ref.at[core * near + j],
+                        tile_send.at[0],
+                        tile_recv.at[0],
+                        {"mem": y * CORES + user, **tile_peer(j - REACH)},
+                    ).start()
+        remote(
+            stage_ref.at[REACH, :, 1 - core],
+            near_ref.at[core * near + REACH],
+            tile_send.at[0],
+            tile_recv.at[0],
+            {"mem": sibling},
+        ).start()
+
+    @pl.when(both(wraps, me >= CORES))
+    def _():
+        enter()
+
+    head = pieces[0][2]
+    ens_copy(0).wait()
     head_bytes = 4 * columns * (members + 2)
     drain(acc_ref.at[pl.ds(0, head_bytes // 512)], in_sem.at[0])
-    mix_block(0)
-
-    @pl.when(jnp.logical_not(gate))
-    def _():
-        pl.semaphore_wait(barrier, n_mem - 1)
-        pl.semaphore_signal(hello, inc=1, device_id={"mem": GATE}, device_id_type=MESH)
+    mix_part(0, 0, head)
+
+    @pl.when(jnp.logical_not(wraps))
+    def _():
+        pl.semaphore_wait(barrier, n_mem - 1 + 2 * REACH * CORES)
+
+    @pl.when(both(wraps, both(me < CORES, me != GATE)))
+    def _():
+        enter()
+
+    @pl.when(jnp.logical_not(both(wraps, gate)))
+    def _():
         own_fc(0)
 
+    mix_part(0, head, fields)
+
     def mix(step, carry):
-        mix_block(step)
+        ens_copy(step).wait()
+        mix_part(step, 0, fields)
         return carry
 
     lax.fori_loop(1, n_mem, mix, 0)
 
-    @pl.when(gate)
+    drain(slot_ref.at[pl.ds(0, CORES * (near + 2))], in_sem.at[2])
+
+    @pl.when(jnp.logical_not(wraps))
+    def _():
+        send_weights()
+
+    @pl.when(both(wraps, gate))
     def _():
         pl.semaphore_wait(hello, n_mem - 1)
-        for offset in range(-REACH, REACH + 1):
-            if offset:
-                pl.semaphore_signal(
-                    barrier, inc=1, device_id=tile_peer(offset), device_id_type=MESH
-                )
         own_fc(0)
 
-    drain(slot_ref.at[pl.ds(0, 2)], in_sem.at[1])
+    drain(slot_ref.at[pl.ds(0, 2 * CORES)], in_sem.at[1])
     share = slots // CHUNKS
     width = min(share, 512)
     flat = jnp.concatenate(
@@ -372,110 +437,118 @@
         own_seen(h)
 
     n_pieces = len(pieces)
-    for piece in range(1, n_pieces):
+    for piece in range(1, n_pieces - 2):
         own_fc(piece)
 
-    @pl.when(gate)
-    def _():
-        pl.semaphore_wait(barrier, 2 * REACH)
+    @pl.when(both(wraps, gate))
+    def _():
+        pl.semaphore_wait(barrier, 2 * REACH * n_mem)
         for step in range(1, n_mem):
             pl.semaphore_signal(
                 ready, inc=1, device_id={"mem": lax.rem(me + step, n_mem)}, device_id_type=MESH
             )
 
-    @pl.when(jnp.logical_not(gate))
+    @pl.when(both(wraps, jnp.logical_not(gate)))
     def _():
         pl.semaphore_wait(ready, 1)
 
-    for j in range(near):
+    @pl.when(wraps)
+    def _():
+        send_weights()
+
+    rounds = CHUNKS // CORES
+    lanes = 128
+    base = [
+        valid_ref[i, core].astype(jnp.float32) / error_ref[i, core].astype(jnp.float32)
+        for i in range(rounds)
+    ]
+    for i in range(rounds):
+        slot_ref[CORES * near, i] = value_ref[i, core].astype(jnp.float32)
+        for spare in range(CORES * near + 1, slot_ref.shape[0]):
+            slot_ref[spare, i] = jnp.zeros_like(base[i])
+    near_ref[core * near + REACH] = stage_ref[REACH, :, core]
+
+    relay_fc(0)
+
+    drain(near_ref.at[pl.ds(0, CORES * near - 1)], tile_recv.at[0])
+    for r in range(CORES * near):
+        for i in range(rounds):
+            slot_ref[r, i] = base[i] * near_ref[r, i]
+
+    for i in range(rounds):
+        drain(seen_ref.at[pl.ds(0, n_mem - 1), 0], seen_recv.at[i])
+        seen = jnp.concatenate(
+            [seen_ref[m, i * CORES + core].astype(jnp.float32) for m in range(n_mem)], axis=0
+        )
+        average = jnp.mean(seen, axis=0, keepdims=True)
+        deviation = seen - average
+        rinv = jnp.concatenate(
+            [slot_ref[:, i, r, :] for r in range(share // lanes)], axis=1
+        )
+        innovation = rinv[CORES * near : CORES * near + 1] - average
+        right = jnp.concatenate(
+            [deviation, jnp.broadcast_to(innovation, deviation.shape)], axis=0
+        ).astype(jnp.bfloat16)
+        rows = [
+            (deviation * rinv[r : r + 1]).astype(jnp.bfloat16) for r in range(CORES * near)
+        ]
+        sums = lax.dot_general(
+            jnp.concatenate(rows, axis=0),
+            right,
+            (((1,), (1,)), ((), ())),
+            preferred_element_type=jnp.float32,
+        )
+        if i:
+            sums = sums + acc_ref[...]
+        acc_ref[...] = sums
+
+    fold = everyone // 2
+    lane = lax.broadcasted_iota(jnp.int32, (fold, 2 * everyone), 1)
+    for r in range(CORES * near):
+        upper = acc_ref[r * everyone : r * everyone + fold]
+        lower = acc_ref[r * everyone + fold : (r + 1) * everyone]
+        packed = jnp.where(lane < everyone + fold, pltpu.roll(lower, fold, 1), upper)
+        packed = jnp.where(lane < everyone, upper, packed)
+        packed = jnp.where(lane < 2 * everyone - fold // 2, packed, lower)
+        part_ref[r] = packed.astype(jnp.bfloat16)
+        user, j = r // near, r % near
         if j != REACH:
             remote(
-                weight_hbm.at[j],
-                near_ref.at[j],
-                tile_send.at[0],
-                tile_recv.at[0],
-                tile_peer(j - REACH),
-            ).start()
-    drain(slot_ref.at[pl.ds(0, 3)], in_sem.at[2])
-    base = valid_ref[...].astype(jnp.float32) / error_ref[...].astype(jnp.float32)
-    slot_ref[near] = value_ref[...].astype(jnp.float32)
-    for spare in range(near + 1, slot_ref.shape[0]):
-        slot_ref[spare] = jnp.zeros_like(base)
-    slot_ref[REACH] = base * near_ref[REACH]
-    acc_ref[...] = jnp.zeros_like(acc_ref)
-
-    relay_fc(0)
-    lanes = 128
-
-    relay_seen(0)
-    relay_seen(1)
-
-    drain(near_ref.at[pl.ds(0, near - 1)], tile_recv.at[0])
-    for j in range(near):
-        if j != REACH:
-            slot_ref[j] = base * near_ref[j]
-
-    for h in range(CHUNKS):
-        if h >= 1 and h + 1 < CHUNKS:
-            relay_seen(h + 1)
-        drain(seen_ref.at[pl.ds(0, n_y), h], seen_all.at[h])
-
-        def gather_stats(step, carry, h=h):
-            inner = pl.ds(pl.multiple_of(step * width, width), width)
-            seen = jnp.concatenate(
-                [seen_ref[m, h, :, inner].astype(jnp.float32) for m in range(n_mem)], axis=0
-            )
-            average = jnp.mean(seen, axis=0, keepdims=True)
-            deviation = seen - average
-            first = (h * share + step * width) // lanes
-            rinv = jnp.concatenate(
-                [slot_ref[:, first + r, :] for r in range(width // lanes)], axis=1
-            )
-            innovation = rinv[near : near + 1] - average
-            pulls = rinv * innovation
-            rows = [(deviation * rinv[j : j + 1]).astype(jnp.bfloat16) for j in range(near)]
-            rows.append(jnp.concatenate([pulls, jnp.zeros_like(pulls)], axis=0).astype(jnp.bfloat16))
-            sums = lax.dot_general(
-                jnp.concatenate(rows, axis=0),
-                deviation.astype(jnp.bfloat16),
-                (((1,), (1,)), ((), ())),
-                preferred_element_type=jnp.float32,
-            )
-            acc_ref[:, :everyone] += sums
-            return carry
-
-        lax.fori_loop(0, share // width, gather_stats, 0)
-
-    fold = everyone // 2
-    for j in range(near):
-        sums = acc_ref[j * everyone : (j + 1) * everyone, :everyone]
-        part_ref[j, :fold] = jnp.concatenate([sums[:fold], sums[fold:]], axis=1)
-        part_ref[j, fold:] = jnp.broadcast_to(
-            acc_ref[near * everyone + j : near * everyone + j + 1], (8, 2 * everyone)
-        )
-
-    for j in range(near):
-        if j != REACH:
-            remote(
-                part_ref.at[j],
-                got_ref.at[j],
+                part_ref.at[r],
+                got_ref.at[core * near + j],
                 tile_send.at[1],
                 tile_recv.at[1],
-                tile_peer(REACH - j),
+                {"mem": y * CORES + user, **tile_peer(REACH - j)},
             ).start()
+    remote(
+        part_ref.at[(1 - core) * near + REACH],
+        got_ref.at[core * near + REACH],
+        tile_send.at[1],
+        tile_recv.at[1],
+        {"mem": sibling},
+    ).start()
+    got_ref[core * near + REACH] = part_ref[core * near + REACH]
 
     relay_fc(1)
-    relay_fc(2)
-
-    summed = part_ref[REACH]
-    drain(got_ref.at[pl.ds(0, near - 1)], tile_recv.at[1])
-
-    for j in range(near):
-        if j != REACH:
-            summed = summed + got_ref[j]
+
+    drain(got_ref.at[pl.ds(0, CORES * near - 1)], tile_recv.at[1])
+
+    summed = got_ref[0].astype(jnp.float32)
+    for r in range(1, CORES * near):
+        summed = summed + got_ref[r].astype(jnp.float32)
     summed = summed / (everyone - 1.0)
-    spread = jnp.concatenate([summed[:fold, :everyone], summed[:fold, everyone:]], axis=0)
-    pulled = summed[fold:, :everyone]
+    flipped = jnp.transpose(summed)
+    spread = jnp.concatenate(
+        [
+            summed[:, :everyone],
+            jnp.concatenate(
+                [flipped[fold:everyone], summed[:, everyone : everyone + fold]], axis=1
+            ),
+        ],
+        axis=0,
+    )
+    first, second = everyone + fold, 2 * everyone - fold // 2
+    pulled = jnp.concatenate([flipped[first : first + 8], flipped[second : second + 8]], axis=1)
     rows = lax.broadcasted_iota(jnp.int32, (everyone, everyone), 0)
     identity = jnp.where(
         rows == lax.broadcasted_iota(jnp.int32, (everyone, everyone), 1), 1.0, 0.0
@@ -515,15 +588,17 @@
             t_recv.at[0],
             {"mem": target},
         ).start()
+    own_fc(n_pieces - 2)
+    finish_fc(n_pieces - 1)
     trecv_ref[me] = tsend_ref[me]
 
     group = 8
 
-    def apply(block):
+    def apply(block, start, stop):
         where = pl.ds(block * wide, wide)
         left = jnp.concatenate(halves(trecv_ref[block][:, :everyone]), axis=0)
         land = jnp.broadcast_to(land_ref[:, where], (members, wide)) > 0
-        for first in range(0, fields, group):
+        for first in range(start, stop, group):
             states = jnp.concatenate(
                 [
                     jnp.concatenate([fc_ref[m, block, f] for m in range(n_mem)], axis=0)
@@ -531,31 +606,34 @@
                 ],
                 axis=1,
             )
-            both = rounded_dot(left, states)
-            total = both[:members] + both[members:]
+            pair = rounded_dot(left, states)
+            total = pair[:members] + pair[members:]
             for f in range(group):
                 moved_ref[first + f, :, :] = jnp.where(
                     land,
                     total[:, f * wide : (f + 1) * wide],
                     fc_ref[me, block, first + f].astype(jnp.float32),
                 )
-        out_ref[:, :, where] = jnp.transpose(moved_ref[...], (1, 0, 2)).astype(jnp.bfloat16)
-
-    for piece in range(3, n_pieces - 1):
+        moved = jnp.transpose(moved_ref[start:stop], (1, 0, 2)).astype(jnp.bfloat16)
+        out_ref[:, start:stop, where] = moved
+
+    for piece in range(2, n_pieces - 2):
         relay_fc(piece)
 
     drain(trecv_ref.at[pl.ds(0, n_mem - 1)], t_recv.at[0])
 
-    for block in range(n_mem):
-        if block == n_mem - 2:
-            relay_fc(n_pieces - 1)
-        drain(fc_ref.at[pl.ds(0, n_y), block], fc_block.at[block])
-        apply(block)
+    for unit, (block, start, stop) in enumerate(units):
+        if unit == 1:
+            relay_fc(n_pieces - 2)
+        count = n_y if unit < len(units) - 1 else n_mem - 1
+        drain(fc_ref.at[pl.ds(0, count), block, pl.ds(start, stop - start)], fc_unit.at[unit])
+        apply(block, start, stop)
 
     drain(fc_ref.at[pl.ds(0, n_mem - 1)], fc_send.at[0])
-    drain(seen_ref.at[pl.ds(0, n_mem - 1)], seen_send.at[0])
-    drain(near_ref.at[pl.ds(0, near - 1)], tile_send.at[0])
-    drain(part_ref.at[pl.ds(0, near - 1)], tile_send.at[1])
+    drain(seen_ref.at[pl.ds(0, n_y - 1)], seen_send.at[0])
+    drain(seen_ref.at[0, pl.ds(0, CHUNKS // CORES)], seen_send.at[1])
+    drain(near_ref.at[pl.ds(0, CORES * near - 1)], tile_send.at[0])
+    drain(part_ref.at[pl.ds(0, CORES * near - 1)], tile_send.at[1])
     drain(tsend_ref.at[pl.ds(0, n_mem - 1)], t_send.at[0])
 
 
@@ -580,15 +658,17 @@
     n_y = n_mem // CORES
     wide = columns // n_mem
     half = fields // 2
-    pieces = [(0, 0, half), (0, half, fields)]
-    pieces += [(block, 0, fields) for block in range(1, n_mem - 1)]
-    pieces += [(n_mem - 1, 0, half), (n_mem - 1, half, fields)]
+    units = [(block, 0, fields) for block in range(n_mem - 1)]
+    cuts = (0, fields - 16, fields - 8, fields)
+    units += [(n_mem - 1, *ends) for ends in zip(cuts[:-1], cuts[1:])]
+    pieces = [(0, 0, half, 0), (0, half, fields, 0)]
+    pieces += [(*unit, index) for index, unit in enumerate(units) if index]
     row = lambda a: a.reshape(1, -1)
-    table = lambda a: a.reshape(-1, 128)
+    table = (CHUNKS // CORES, CORES, slots // CHUNKS // 128, 128)
     far = pl.BlockSpec(memory_space=pltpu.HBM)
     dma = pltpu.SemaphoreType.DMA
     return pl.pallas_call(
-        functools.partial(kernel, n_mem, n_tile, pieces),
+        functools.partial(kernel, n_mem, n_tile, pieces, units),
         out_shape=pltpu.VMEM(ensemble_profiles_before.shape, jnp.bfloat16),
         in_specs=[far] * 10,
         out_specs=pl.BlockSpec(memory_space=pltpu.VMEM),
@@ -599,27 +679,27 @@
             pltpu.VMEM((1, columns), jnp.int32),
             pltpu.VMEM((1, slots), jnp.int32),
             pltpu.VMEM((1, slots), jnp.int32),
-            pltpu.VMEM((slots // 128, 128), jnp.int32),
-            pltpu.VMEM((slots // 128, 128), jnp.bfloat16),
-            pltpu.VMEM((slots // 128, 128), jnp.bfloat16),
+            pltpu.VMEM(table, jnp.int32),
+            pltpu.VMEM(table, jnp.bfloat16),
+            pltpu.VMEM(table, jnp.bfloat16),
             pltpu.VMEM((n_mem, n_mem, fields, members, wide), jnp.bfloat16),
             pltpu.VMEM((n_mem, CHUNKS, members, slots // CHUNKS), jnp.bfloat16),
-            pltpu.VMEM((near, slots // 128, 128), jnp.float32),
-            pltpu.VMEM((8, slots // 128, 128), jnp.float32),
-            pltpu.VMEM((near * everyone + 16, 2 * everyone), jnp.float32),
-            pltpu.VMEM((near, everyone // 2 + 8, 2 * everyone), jnp.float32),
-            pltpu.VMEM((near, everyone // 2 + 8, 2 * everyone), jnp.float32),
+            pltpu.VMEM((near, *table), jnp.float32),
+            pltpu.VMEM((CORES * near, table[0], *table[2:]), jnp.float32),
+            pltpu.VMEM((16, table[0], *table[2:]), jnp.float32),
+            pltpu.VMEM((CORES * near * everyone, 2 * everyone), jnp.float32),
+            pltpu.VMEM((CORES * near, everyone // 2, 2 * everyone), jnp.bfloat16),
+            pltpu.VMEM((CORES * near, everyone // 2, 2 * everyone), jnp.bfloat16),
             pltpu.VMEM((n_mem, members, 2 * everyone), jnp.float32),
             pltpu.VMEM((n_mem, members, 2 * everyone), jnp.float32),
             pltpu.VMEM((fields, members, wide), jnp.float32),
             dma((n_mem,)),
             dma((3,)),
+            dma((2,)),
+            dma((CHUNKS // CORES,)),
             dma((1,)),
-            dma((CHUNKS, n_y - 1)),
-            dma((CHUNKS,)),
-            dma((1,)),
-            dma((len(pieces), n_y - 1)),
-            dma((n_mem,)),
+            dma((len(pieces) - 1, n_y - 1)),
+            dma((len(units),)),
             dma((2,)),
             dma((2,)),
             dma((1,)),
@@ -637,10 +717,10 @@
         row(terrain_indicator),
         row(measured_profile_position),
         row(measured_field_index),
-        table(obs_valid),
-        table(obs_value),
-        table(obs_error),
-        local_weight.reshape(near, slots // 128, 128),
+        obs_valid.reshape(table),
+        obs_value.reshape(table),
+        obs_error.reshape(table),
+        local_weight.reshape(near, *table),
     )
 
 
@@ -653,8 +733,9 @@
         and n_tile > 2 * REACH
         and members % 16 == 0
         and fields % 8 == 0
+        and fields > 16
         and columns % (128 * n_mem) == 0
-        and slots // n_tile % (512 * CHUNKS) == 0
+        and slots // n_tile % (1024 * CHUNKS) == 0
     )
 
 

time: 27.3 us -> 25.2 us (0.923)
  Pallas kernels: 26.3 us -> 24.3 us
    pallas_call x1, Pallas kernels: 26.3 us -> 24.3 us  [on_device(): pl.pallas_call(functools.partial(kernel, n_mem, n_tile, pieces, units), o...]
where the time goes in v2:
time: 25.2 us; the launch traced here: 25.1 us
  Pallas kernels  24.3 us (96%)
  local copies, waits for them, and re-layouts  0.84 us (3%)
    pallas_call x1, Pallas kernels, on_device(): pl.pallas_call(functools.partial(kernel, n_mem, n_tile, pieces, units), o...  24.3 us
    unnamed x1, local copies, waits for them, and re-layouts  0.84 us

profile of v2, /device:TPU:0, one launch (start us, length us, event | category | flops | bytes accessed | tf_op | source)
XLA Modules:
  0.0 25.1 jit_solution(10988399524575670634)
XLA Ops:
  0.0 24.3 %shard_map.100 = bf16[16,40,512]{2,1,0:T(8,128)(2,1)S(1)} custom-call(bf16[16,40,512]{2,1,0:T(8,128)(2,1)} %ens_hbm.1, f32[1,512]{1,0:T(1,128)} %bitcast.14, f32[16,512]{1,0:T(8,128)} %surf_hbm.1, s32[1,512]{1,0:T(1,128)} %bitcast.15, s32[1,4096]{1,0:T(1,128)} %bitcast.9, s32[1,4096]{1,0:T(1,128)} %bitcast.10, s32[2,2,8,128]{3,2,1,0:T(8,128)} %bitcast.11, ...), custom_call_target="tpu_custom_call" | custom-call | tf_op jit(solution)/shard_map/pallas_call | solution.py:670
  24.3 0.8 %copy.12 = bf16[16,40,512]{2,1,0:T(8,128)(2,1)} copy(bf16[16,40,512]{2,1,0:T(8,128)(2,1)S(1)} %shard_map.100) | data formatting | bytes 1310720

commit v3 on v2

--- a/solution.py
+++ b/solution.py
@@ -198,6 +198,7 @@
     stage_ref,
     near_ref,
     slot_ref,
+    rinv_ref,
     acc_ref,
     part_ref,
     got_ref,
@@ -329,9 +330,11 @@
         for step in range(1, n_y):
             seen_copy(h, 0, lax.rem(y + step, n_y) * CORES + user).start()
 
-        @pl.when(core != user)
-        def _():
-            seen_copy(h, 1, sibling).start()
+    def near_seen():
+        for i in range(CHUNKS // CORES):
+            h = i * CORES + 1 - core
+            ref = seen_ref.at[me, h]
+            remote(ref, ref, seen_send.at[1], seen_recv.at[i], {"mem": sibling}).start()
 
     def tile_peer(offset):
         return {"tile": lax.rem(tile + offset + n_tile, n_tile)}
@@ -399,6 +402,10 @@
 
     mix_part(0, head, fields)
 
+    @pl.when(jnp.logical_not(both(wraps, gate)))
+    def _():
+        own_fc(1)
+
     def mix(step, carry):
         ens_copy(step).wait()
         mix_part(step, 0, fields)
@@ -416,6 +423,7 @@
     def _():
         pl.semaphore_wait(hello, n_mem - 1)
         own_fc(0)
+        own_fc(1)
 
     drain(slot_ref.at[pl.ds(0, 2 * CORES)], in_sem.at[1])
     share = slots // CHUNKS
@@ -434,10 +442,13 @@
             for f in range(1, fields):
                 total = jnp.where(wanted == f, found[f * members : (f + 1) * members], total)
             seen_ref[me, h, :, pl.ds(step * width, width)] = total.astype(jnp.bfloat16)
-        own_seen(h)
-
+        if h % CORES == CORES - 1:
+            for done in range(h + 1 - CORES, h + 1):
+                own_seen(done)
+
+    near_seen()
     n_pieces = len(pieces)
-    for piece in range(1, n_pieces - 2):
+    for piece in range(2, n_pieces - 2):
         own_fc(piece)
 
     @pl.when(both(wraps, gate))
@@ -469,11 +480,15 @@
     near_ref[core * near + REACH] = stage_ref[REACH, :, core]
 
     relay_fc(0)
+    relay_fc(1)
 
     drain(near_ref.at[pl.ds(0, CORES * near - 1)], tile_recv.at[0])
     for r in range(CORES * near):
         for i in range(rounds):
             slot_ref[r, i] = base[i] * near_ref[r, i]
+    for i in range(rounds):
+        for r in range(share // lanes):
+            rinv_ref[i, :, r * lanes : (r + 1) * lanes] = slot_ref[:, i, r, :]
 
     for i in range(rounds):
         drain(seen_ref.at[pl.ds(0, n_mem - 1), 0], seen_recv.at[i])
@@ -482,9 +497,7 @@
         )
         average = jnp.mean(seen, axis=0, keepdims=True)
         deviation = seen - average
-        rinv = jnp.concatenate(
-            [slot_ref[:, i, r, :] for r in range(share // lanes)], axis=1
-        )
+        rinv = rinv_ref[i]
         innovation = rinv[CORES * near : CORES * near + 1] - average
         right = jnp.concatenate(
             [deviation, jnp.broadcast_to(innovation, deviation.shape)], axis=0
@@ -492,15 +505,15 @@
         rows = [
             (deviation * rinv[r : r + 1]).astype(jnp.bfloat16) for r in range(CORES * near)
         ]
-        sums = lax.dot_general(
-            jnp.concatenate(rows, axis=0),
-            right,
-            (((1,), (1,)), ((), ())),
-            preferred_element_type=jnp.float32,
-        )
-        if i:
-            sums = sums + acc_ref[...]
-        acc_ref[...] = sums
+        for user in range(CORES):
+            where = slice(user * near * everyone, (user + 1) * near * everyone)
+            sums = lax.dot_general(
+                jnp.concatenate(rows[user * near : (user + 1) * near], axis=0),
+                right,
+                (((1,), (1,)), ((), ())),
+                preferred_element_type=jnp.float32,
+            )
+            acc_ref[where] = sums + acc_ref[where] if i else sums
 
     fold = everyone // 2
     lane = lax.broadcasted_iota(jnp.int32, (fold, 2 * everyone), 1)
@@ -529,7 +542,7 @@
     ).start()
     got_ref[core * near + REACH] = part_ref[core * near + REACH]
 
-    relay_fc(1)
+    relay_fc(2)
 
     drain(got_ref.at[pl.ds(0, CORES * near - 1)], tile_recv.at[1])
 
@@ -617,7 +630,7 @@
         moved = jnp.transpose(moved_ref[start:stop], (1, 0, 2)).astype(jnp.bfloat16)
         out_ref[:, start:stop, where] = moved
 
-    for piece in range(2, n_pieces - 2):
+    for piece in range(3, n_pieces - 2):
         relay_fc(piece)
 
     drain(trecv_ref.at[pl.ds(0, n_mem - 1)], t_recv.at[0])
@@ -661,7 +674,7 @@
     units = [(block, 0, fields) for block in range(n_mem - 1)]
     cuts = (0, fields - 16, fields - 8, fields)
     units += [(n_mem - 1, *ends) for ends in zip(cuts[:-1], cuts[1:])]
-    pieces = [(0, 0, half, 0), (0, half, fields, 0)]
+    pieces = [(0, 0, 16, 0), (0, 16, half + 8, 0), (0, half + 8, fields, 0)]
     pieces += [(*unit, index) for index, unit in enumerate(units) if index]
     row = lambda a: a.reshape(1, -1)
     table = (CHUNKS // CORES, CORES, slots // CHUNKS // 128, 128)
@@ -687,6 +700,7 @@
             pltpu.VMEM((near, *table), jnp.float32),
             pltpu.VMEM((CORES * near, table[0], *table[2:]), jnp.float32),
             pltpu.VMEM((16, table[0], *table[2:]), jnp.float32),
+            pltpu.VMEM((table[0], 16, slots // CHUNKS), jnp.float32),
             pltpu.VMEM((CORES * near * everyone, 2 * everyone), jnp.float32),
             pltpu.VMEM((CORES * near, everyone // 2, 2 * everyone), jnp.bfloat16),
             pltpu.VMEM((CORES * near, everyone // 2, 2 * everyone), jnp.bfloat16),
@@ -733,7 +747,7 @@
         and n_tile > 2 * REACH
         and members % 16 == 0
         and fields % 8 == 0
-        and fields > 16
+        and fields > 32
         and columns % (128 * n_mem) == 0
         and slots // n_tile % (1024 * CHUNKS) == 0
     )

time: 25.2 us -> 24.2 us (0.960)
  Pallas kernels: 24.3 us -> 23.2 us
    pallas_call x1, Pallas kernels: 24.3 us -> 23.2 us  [on_device(): pl.pallas_call(functools.partial(kernel, n_mem, n_tile, pieces, units), o...]
where the time goes in v3:
time: 24.2 us; the launch traced here: 24.1 us
  Pallas kernels  23.2 us (96%)
  local copies, waits for them, and re-layouts  0.84 us (3%)
    pallas_call x1, Pallas kernels, on_device(): pl.pallas_call(functools.partial(kernel, n_mem, n_tile, pieces, units), o...  23.2 us
    unnamed x1, local copies, waits for them, and re-layouts  0.84 us

profile of v3, /device:TPU:0, one launch (start us, length us, event | category | flops | bytes accessed | tf_op | source)
XLA Modules:
  0.0 24.1 jit_solution(6654246140598190372)
XLA Ops:
  0.0 23.2 %shard_map.100 = bf16[16,40,512]{2,1,0:T(8,128)(2,1)S(1)} custom-call(bf16[16,40,512]{2,1,0:T(8,128)(2,1)} %ens_hbm.1, f32[1,512]{1,0:T(1,128)} %bitcast.14, f32[16,512]{1,0:T(8,128)} %surf_hbm.1, s32[1,512]{1,0:T(1,128)} %bitcast.15, s32[1,4096]{1,0:T(1,128)} %bitcast.9, s32[1,4096]{1,0:T(1,128)} %bitcast.10, s32[2,2,8,128]{3,2,1,0:T(8,128)} %bitcast.11, ...), custom_call_target="tpu_custom_call" | custom-call | tf_op jit(solution)/shard_map/pallas_call | solution.py:683
  23.2 0.8 %copy.12 = bf16[16,40,512]{2,1,0:T(8,128)(2,1)} copy(bf16[16,40,512]{2,1,0:T(8,128)(2,1)S(1)} %shard_map.100) | data formatting | bytes 1310720

commit v4 on v3

--- a/solution.py
+++ b/solution.py
@@ -1,4 +1,5 @@
 import functools
+import math
 
 import jax
 import jax.numpy as jnp
@@ -166,6 +167,13 @@
 
 def drain(ref, sem):
     pltpu.make_async_copy(ref, ref, sem).wait()
+
+
+def counter(bytes_ref):
+    def count(size, sem):
+        drain(bytes_ref.at[pl.ds(0, size // 512)], sem)
+
+    return count
 
 
 def kernel(
@@ -205,16 +213,14 @@
     tsend_ref,
     trecv_ref,
     moved_ref,
+    bytes_ref,
     ens_sem,
     in_sem,
-    seen_send,
+    out_sem,
     seen_recv,
-    fc_send,
     fc_across,
     fc_unit,
-    tile_send,
     tile_recv,
-    t_send,
     t_recv,
     hello,
     ready,
@@ -224,6 +230,7 @@
     slots = pos_ref.shape[1]
     near = 2 * REACH + 1
     wide = columns // n_mem
+    count = counter(bytes_ref)
     me, tile = lax.axis_index("mem"), lax.axis_index("tile")
     n_y = n_mem // CORES
     y, core = me // CORES, lax.rem(me, CORES)
@@ -239,27 +246,21 @@
     for step in range(1, n_mem):
         peer = lax.rem(me + step, n_mem)
 
-        @pl.when(jnp.logical_not(both(wraps, peer == GATE)))
+        @pl.when(peer != GATE)
         def _(peer=peer):
             pl.semaphore_signal(barrier, inc=1, device_id={"mem": peer}, device_id_type=MESH)
 
     for offset in range(-REACH, REACH + 1):
         if offset:
             there = lax.rem(tile + offset + n_tile, n_tile)
-            for user in range(CORES):
-                who = y * CORES + user
-
-                @pl.when(jnp.logical_or(there >= REACH, user == 0))
-                def _(there=there, who=who):
-                    target = jnp.where(there < REACH, GATE, who)
-                    pl.semaphore_signal(
-                        barrier, inc=1, device_id={"mem": target, "tile": there}, device_id_type=MESH
-                    )
+            pl.semaphore_signal(
+                barrier, inc=1, device_id={"mem": GATE, "tile": there}, device_id_type=MESH
+            )
 
     def ens_copy(step):
         where = pl.ds(pl.multiple_of(step * wide, wide), wide)
         return pltpu.make_async_copy(
-            ens_hbm.at[:, :, where], ens_ref.at[:, :, where], ens_sem.at[step]
+            ens_hbm.at[:, :, where], ens_ref.at[:, :, where], ens_sem.at[min(step, 1)]
         )
 
     groups = [
@@ -273,7 +274,7 @@
         ],
     ]
     loads = [
-        [pltpu.make_async_copy(src, dst, in_sem.at[g]) for src, dst in group]
+        [pltpu.make_async_copy(src, dst, in_sem.at[min(g, 1)]) for src, dst in group]
         for g, group in enumerate(groups)
     ]
     ens_copy(0).start()
@@ -298,18 +299,17 @@
     def fc_copy(piece, owner, recv, target):
         block, first, stop = pieces[piece][:3]
         ref = fc_ref.at[owner, block, pl.ds(first, stop - first)]
-        return remote(ref, ref, fc_send.at[0], recv, {"mem": target})
+        return remote(ref, ref, out_sem.at[0], recv, {"mem": target})
 
     def fc_over(piece, owner, index, target):
-        return fc_copy(piece, owner, fc_across.at[piece, index], target)
+        return fc_copy(piece, owner, fc_across.at[max(piece - 2, piece // 2), index], target)
 
     def fc_near(piece, owner):
-        return fc_copy(piece, owner, fc_unit.at[pieces[piece][3]], sibling)
+        return fc_copy(piece, owner, fc_unit.at[max(pieces[piece][3] + 3 - len(units), 0)], sibling)
 
     def finish_fc(piece):
         for step in range(1, n_mem):
-            unit = fc_unit.at[pieces[piece][3]]
-            fc_copy(piece, me, unit, lax.rem(me + step, n_mem)).start()
+            fc_copy(piece, me, fc_unit.at[2], lax.rem(me + step, n_mem)).start()
 
     def own_fc(piece):
         for index, peer in enumerate(across):
@@ -321,20 +321,20 @@
             fc_over(piece, peer, index, peer).wait_recv()
             fc_near(piece, peer).start()
 
-    def seen_copy(h, send, target):
+    def seen_copy(h, target):
         ref = seen_ref.at[me, h]
-        return remote(ref, ref, seen_send.at[send], seen_recv.at[h // CORES], {"mem": target})
+        return remote(ref, ref, out_sem.at[0], seen_recv.at[h // CORES], {"mem": target})
 
     def own_seen(h):
         user = h % CORES
         for step in range(1, n_y):
-            seen_copy(h, 0, lax.rem(y + step, n_y) * CORES + user).start()
+            seen_copy(h, lax.rem(y + step, n_y) * CORES + user).start()
 
     def near_seen():
         for i in range(CHUNKS // CORES):
             h = i * CORES + 1 - core
             ref = seen_ref.at[me, h]
-            remote(ref, ref, seen_send.at[1], seen_recv.at[i], {"mem": sibling}).start()
+            remote(ref, ref, out_sem.at[0], seen_recv.at[i], {"mem": sibling}).start()
 
     def tile_peer(offset):
         return {"tile": lax.rem(tile + offset + n_tile, n_tile)}
@@ -366,66 +366,78 @@
                     remote(
                         stage_ref.at[j, :, user],
                         near_ref.at[core * near + j],
-                        tile_send.at[0],
+                        out_sem.at[0],
                         tile_recv.at[0],
                         {"mem": y * CORES + user, **tile_peer(j - REACH)},
                     ).start()
         remote(
             stage_ref.at[REACH, :, 1 - core],
             near_ref.at[core * near + REACH],
-            tile_send.at[0],
+            out_sem.at[0],
             tile_recv.at[0],
             {"mem": sibling},
         ).start()
 
-    @pl.when(both(wraps, me >= CORES))
+    def admit():
+        pl.semaphore_wait(barrier, 2 * REACH * n_mem)
+        for step in range(1, n_mem):
+            peer = lax.rem(me + step, n_mem)
+            pl.semaphore_signal(ready, inc=1, device_id={"mem": peer}, device_id_type=MESH)
+
+    def meet_tiles():
+        @pl.when(both(wraps, gate))
+        def _():
+            admit()
+
+        @pl.when(jnp.logical_not(gate))
+        def _():
+            pl.semaphore_wait(ready, 1)
+
+        send_weights()
+
+    @pl.when(me >= CORES)
     def _():
         enter()
 
     head = pieces[0][2]
     ens_copy(0).wait()
-    head_bytes = 4 * columns * (members + 2)
-    drain(acc_ref.at[pl.ds(0, head_bytes // 512)], in_sem.at[0])
+    count(4 * columns * (members + 2), in_sem.at[0])
     mix_part(0, 0, head)
 
-    @pl.when(jnp.logical_not(wraps))
-    def _():
-        pl.semaphore_wait(barrier, n_mem - 1 + 2 * REACH * CORES)
-
-    @pl.when(both(wraps, both(me < CORES, me != GATE)))
+    @pl.when(both(me < CORES, me != GATE))
     def _():
         enter()
 
-    @pl.when(jnp.logical_not(both(wraps, gate)))
+    @pl.when(me != GATE)
     def _():
         own_fc(0)
 
     mix_part(0, head, fields)
 
-    @pl.when(jnp.logical_not(both(wraps, gate)))
+    @pl.when(me != GATE)
     def _():
         own_fc(1)
 
+    count(2 * members * fields * wide * (n_mem - 1), ens_sem.at[1])
+
     def mix(step, carry):
-        ens_copy(step).wait()
         mix_part(step, 0, fields)
         return carry
 
     lax.fori_loop(1, n_mem, mix, 0)
 
-    drain(slot_ref.at[pl.ds(0, CORES * (near + 2))], in_sem.at[2])
-
-    @pl.when(jnp.logical_not(wraps))
-    def _():
-        send_weights()
-
-    @pl.when(both(wraps, gate))
+    count(4 * slots * (near + 4), in_sem.at[1])
+
+    @pl.when(gate)
     def _():
         pl.semaphore_wait(hello, n_mem - 1)
         own_fc(0)
         own_fc(1)
 
-    drain(slot_ref.at[pl.ds(0, 2 * CORES)], in_sem.at[1])
+    @pl.when(both(gate, jnp.logical_not(wraps)))
+    def _():
+        admit()
+
     share = slots // CHUNKS
     width = min(share, 512)
     flat = jnp.concatenate(
@@ -445,27 +457,22 @@
         if h % CORES == CORES - 1:
             for done in range(h + 1 - CORES, h + 1):
                 own_seen(done)
+            if h < CORES:
+                own_fc(2)
+        if h == 0:
+
+            @pl.when(jnp.logical_not(wraps))
+            def _():
+                meet_tiles()
 
     near_seen()
     n_pieces = len(pieces)
-    for piece in range(2, n_pieces - 2):
+    for piece in range(3, n_pieces - 1):
         own_fc(piece)
-
-    @pl.when(both(wraps, gate))
-    def _():
-        pl.semaphore_wait(barrier, 2 * REACH * n_mem)
-        for step in range(1, n_mem):
-            pl.semaphore_signal(
-                ready, inc=1, device_id={"mem": lax.rem(me + step, n_mem)}, device_id_type=MESH
-            )
-
-    @pl.when(both(wraps, jnp.logical_not(gate)))
-    def _():
-        pl.semaphore_wait(ready, 1)
 
     @pl.when(wraps)
     def _():
-        send_weights()
+        meet_tiles()
 
     rounds = CHUNKS // CORES
     lanes = 128
@@ -479,8 +486,10 @@
             slot_ref[spare, i] = jnp.zeros_like(base[i])
     near_ref[core * near + REACH] = stage_ref[REACH, :, core]
 
-    relay_fc(0)
-    relay_fc(1)
+    for index, peer in enumerate(across):
+        drain(fc_ref.at[peer, 0, pl.ds(0, pieces[1][2])], fc_across.at[0, index])
+        fc_near(0, peer).start()
+        fc_near(1, peer).start()
 
     drain(near_ref.at[pl.ds(0, CORES * near - 1)], tile_recv.at[0])
     for r in range(CORES * near):
@@ -529,20 +538,24 @@
             remote(
                 part_ref.at[r],
                 got_ref.at[core * near + j],
-                tile_send.at[1],
+                out_sem.at[0],
                 tile_recv.at[1],
                 {"mem": y * CORES + user, **tile_peer(REACH - j)},
             ).start()
     remote(
         part_ref.at[(1 - core) * near + REACH],
         got_ref.at[core * near + REACH],
-        tile_send.at[1],
+        out_sem.at[0],
         tile_recv.at[1],
         {"mem": sibling},
     ).start()
     got_ref[core * near + REACH] = part_ref[core * near + REACH]
 
-    relay_fc(2)
+    for index, peer in enumerate(across):
+        first, stop = pieces[2][1], pieces[3][2]
+        drain(fc_ref.at[peer, 0, pl.ds(first, stop - first)], fc_across.at[1, index])
+        fc_near(2, peer).start()
+        fc_near(3, peer).start()
 
     drain(got_ref.at[pl.ds(0, CORES * near - 1)], tile_recv.at[1])
 
@@ -569,23 +582,33 @@
     system = identity + spread
     square = jnp.sum(system * system, keepdims=True)
     scale = jnp.sqrt(square)
+    rows = jnp.concatenate([pulled, jnp.ones_like(pulled)], axis=0)
+    powers = [rows]
     parts = halves(system)
     second = fine_dot(parts, parts) / square
+    powers.append(fine_dot(halves(rows), parts) / scale)
     current = system / scale
     parts, second_parts = halves(current), halves(second)
     third = fine_dot(second_parts, parts)
     fourth = fine_dot(second_parts, second_parts)
-    root = 2.25 * identity - 2.4375 * current + 1.6875 * second - 0.5625 * third + 0.0625 * fourth
+    for power in range(2, 6):
+        powers.append(fine_dot(halves(powers[power - 2]), second_parts))
+    weights = (2.25, -2.4375, 1.6875, -0.5625, 0.0625)
+
+    def combine(terms):
+        return sum(weight * term for weight, term in zip(weights, terms))
+
+    root = combine([identity, current, second, third, fourth])
     root_parts = halves(root)
     inner_parts = halves(fine_dot(parts, root_parts))
     outer_parts = halves(fine_dot(root_parts, root_parts))
     root = 1.5 * root - 0.5 * fine_dot(inner_parts, outer_parts)
+    drawn = 1.5 * combine(powers[:5]) - 0.5 * fine_dot(halves(combine(powers[1:])), outer_parts)
     root_parts = halves(root)
     ones = jnp.ones((everyone, everyone), jnp.bfloat16)
     sums = rounded_dot(root_parts[0], ones) + rounded_dot(root_parts[1], ones)
-    drawn = halves(fine_dot(halves(pulled), root_parts))
-    mean_weight = fine_dot(drawn, root_parts)[:1] / scale
-    weight_sum = fine_dot(drawn, halves(sums))[:1] / scale
+    mean_weight = fine_dot(halves(drawn[:8]), root_parts)[:1] / scale
+    weight_sum = jnp.sum(drawn[:1] * drawn[8:9], axis=1, keepdims=True) / scale
     turned = root / jnp.sqrt(scale) + mean_weight
     turned = turned + (1.0 - sums / jnp.sqrt(scale) - weight_sum) / everyone
     for m in range(n_mem):
@@ -597,11 +620,10 @@
         remote(
             tsend_ref.at[target],
             trecv_ref.at[me],
-            t_send.at[0],
+            out_sem.at[0],
             t_recv.at[0],
             {"mem": target},
         ).start()
-    own_fc(n_pieces - 2)
     finish_fc(n_pieces - 1)
     trecv_ref[me] = tsend_ref[me]
 
@@ -612,42 +634,45 @@
         left = jnp.concatenate(halves(trecv_ref[block][:, :everyone]), axis=0)
         land = jnp.broadcast_to(land_ref[:, where], (members, wide)) > 0
         for first in range(start, stop, group):
+            end = min(first + group, stop)
             states = jnp.concatenate(
                 [
                     jnp.concatenate([fc_ref[m, block, f] for m in range(n_mem)], axis=0)
-                    for f in range(first, first + group)
+                    for f in range(first, end)
                 ],
                 axis=1,
             )
             pair = rounded_dot(left, states)
             total = pair[:members] + pair[members:]
-            for f in range(group):
-                moved_ref[first + f, :, :] = jnp.where(
+            for f in range(end - first):
+                moved_ref[block, first + f] = jnp.where(
                     land,
                     total[:, f * wide : (f + 1) * wide],
                     fc_ref[me, block, first + f].astype(jnp.float32),
                 )
-        moved = jnp.transpose(moved_ref[start:stop], (1, 0, 2)).astype(jnp.bfloat16)
+        moved = jnp.transpose(moved_ref[block, start:stop], (1, 0, 2)).astype(jnp.bfloat16)
         out_ref[:, start:stop, where] = moved
 
-    for piece in range(3, n_pieces - 2):
+    for piece in range(4, n_pieces - 1):
         relay_fc(piece)
 
     drain(trecv_ref.at[pl.ds(0, n_mem - 1)], t_recv.at[0])
 
-    for unit, (block, start, stop) in enumerate(units):
-        if unit == 1:
-            relay_fc(n_pieces - 2)
-        count = n_y if unit < len(units) - 1 else n_mem - 1
-        drain(fc_ref.at[pl.ds(0, count), block, pl.ds(start, stop - start)], fc_unit.at[unit])
-        apply(block, start, stop)
-
-    drain(fc_ref.at[pl.ds(0, n_mem - 1)], fc_send.at[0])
-    drain(seen_ref.at[pl.ds(0, n_y - 1)], seen_send.at[0])
-    drain(seen_ref.at[0, pl.ds(0, CHUNKS // CORES)], seen_send.at[1])
-    drain(near_ref.at[pl.ds(0, CORES * near - 1)], tile_send.at[0])
-    drain(part_ref.at[pl.ds(0, CORES * near - 1)], tile_send.at[1])
-    drain(tsend_ref.at[pl.ds(0, n_mem - 1)], t_send.at[0])
+    n_units = len(units)
+    for chosen in (range(n_units - 2), range(n_units - 2, n_units - 1), range(n_units - 1, n_units)):
+        rows = sum(units[unit][2] - units[unit][1] for unit in chosen)
+        owners = n_y if chosen[-1] < n_units - 1 else n_mem - 1
+        count(2 * owners * rows * members * wide, fc_unit.at[chosen[-1] + 3 - n_units])
+        for unit in chosen:
+            apply(*units[unit])
+
+    kinds = [fc_ref.at[0], seen_ref.at[0], part_ref, stage_ref.at[:, :, 0], tsend_ref.at[0]]
+    sizes = [ref.dtype.itemsize * math.prod(ref.shape) for ref in kinds]
+    counts = [n_mem - 1, n_y - 1, 0, 0, n_mem - 1]
+    total = sum(size * count for size, count in zip(sizes, counts))
+    total += sizes[1] // CORES
+    total += (sizes[2] + sizes[3] * CORES) * (CORES * near - 1) // (CORES * near)
+    count(total, out_sem.at[0])
 
 
 def on_device(
@@ -670,12 +695,12 @@
     near = 2 * REACH + 1
     n_y = n_mem // CORES
     wide = columns // n_mem
-    half = fields // 2
     units = [(block, 0, fields) for block in range(n_mem - 1)]
-    cuts = (0, fields - 16, fields - 8, fields)
+    cuts = (0, fields - 16, fields - 4, fields)
     units += [(n_mem - 1, *ends) for ends in zip(cuts[:-1], cuts[1:])]
-    pieces = [(0, 0, 16, 0), (0, 16, half + 8, 0), (0, half + 8, fields, 0)]
+    pieces = [(0, 0, 16, 0), (0, 16, 28, 0), (0, 28, 32, 0), (0, 32, fields, 0)]
     pieces += [(*unit, index) for index, unit in enumerate(units) if index]
+    spare = 8 * everyone * fields * columns
     row = lambda a: a.reshape(1, -1)
     table = (CHUNKS // CORES, CORES, slots // CHUNKS // 128, 128)
     far = pl.BlockSpec(memory_space=pltpu.HBM)
@@ -706,17 +731,15 @@
             pltpu.VMEM((CORES * near, everyone // 2, 2 * everyone), jnp.bfloat16),
             pltpu.VMEM((n_mem, members, 2 * everyone), jnp.float32),
             pltpu.VMEM((n_mem, members, 2 * everyone), jnp.float32),
-            pltpu.VMEM((fields, members, wide), jnp.float32),
-            dma((n_mem,)),
-            dma((3,)),
-            dma((2,)),
-            dma((CHUNKS // CORES,)),
-            dma((1,)),
-            dma((len(pieces) - 1, n_y - 1)),
-            dma((len(units),)),
+            pltpu.VMEM((n_mem, fields, members, wide), jnp.float32),
+            pltpu.VMEM((spare // 512, 128), jnp.float32),
             dma((2,)),
             dma((2,)),
             dma((1,)),
+            dma((CHUNKS // CORES,)),
+            dma((len(pieces) - 3, n_y - 1)),
+            dma((3,)),
+            dma((2,)),
             dma((1,)),
             pltpu.SemaphoreType.REGULAR,
             pltpu.SemaphoreType.REGULAR,

time: 24.2 us -> 24.1 us (level)
  no operation moved by 1% of the time
where the time goes in v4:
time: 24.1 us; the launch traced here: 23.9 us
  Pallas kernels  23 us (95%)
  local copies, waits for them, and re-layouts  0.84 us (3%)
    pallas_call x1, Pallas kernels, on_device(): pl.pallas_call(functools.partial(kernel, n_mem, n_tile, pieces, units), o...  23 us
    unnamed x1, local copies, waits for them, and re-layouts  0.84 us

profile of v4, /device:TPU:0, one launch (start us, length us, event | category | flops | bytes accessed | tf_op | source)
XLA Modules:
  0.0 23.9 jit_solution(9960609215108028176)
XLA Ops:
  0.0 23.0 %shard_map.100 = bf16[16,40,512]{2,1,0:T(8,128)(2,1)S(1)} custom-call(bf16[16,40,512]{2,1,0:T(8,128)(2,1)} %ens_hbm.1, f32[1,512]{1,0:T(1,128)} %bitcast.14, f32[16,512]{1,0:T(8,128)} %surf_hbm.1, s32[1,512]{1,0:T(1,128)} %bitcast.15, s32[1,4096]{1,0:T(1,128)} %bitcast.9, s32[1,4096]{1,0:T(1,128)} %bitcast.10, s32[2,2,8,128]{3,2,1,0:T(8,128)} %bitcast.11, ...), custom_call_target="tpu_custom_call" | custom-call | tf_op jit(solution)/shard_map/pallas_call | solution.py:708
  23.0 0.8 %copy.12 = bf16[16,40,512]{2,1,0:T(8,128)(2,1)} copy(bf16[16,40,512]{2,1,0:T(8,128)(2,1)S(1)} %shard_map.100) | data formatting | bytes 1310720

commit v5 on v4

--- a/solution.py
+++ b/solution.py
@@ -220,6 +220,7 @@
     seen_recv,
     fc_across,
     fc_unit,
+    lift_sem,
     tile_recv,
     t_recv,
     hello,
@@ -296,20 +297,25 @@
             device_id_type=MESH,
         )
 
+    n_pieces = len(pieces)
+    lifted = n_pieces - 2
+
+    def unit_sem(unit):
+        return {len(units) - 1: 1, len(units) - 2: 2}.get(unit, 0)
+
+    def piece_ref(piece, owner):
+        block, first, stop = pieces[piece][:3]
+        return fc_ref.at[owner, block, pl.ds(first, stop - first)]
+
     def fc_copy(piece, owner, recv, target):
-        block, first, stop = pieces[piece][:3]
-        ref = fc_ref.at[owner, block, pl.ds(first, stop - first)]
+        ref = piece_ref(piece, owner)
         return remote(ref, ref, out_sem.at[0], recv, {"mem": target})
 
     def fc_over(piece, owner, index, target):
-        return fc_copy(piece, owner, fc_across.at[max(piece - 2, piece // 2), index], target)
+        return fc_copy(piece, owner, fc_across.at[min(max(piece - 2, piece // 2), lifted - 2), index], target)
 
     def fc_near(piece, owner):
-        return fc_copy(piece, owner, fc_unit.at[max(pieces[piece][3] + 3 - len(units), 0)], sibling)
-
-    def finish_fc(piece):
-        for step in range(1, n_mem):
-            fc_copy(piece, me, fc_unit.at[2], lax.rem(me + step, n_mem)).start()
+        return fc_copy(piece, owner, fc_unit.at[unit_sem(pieces[piece][3])], sibling)
 
     def own_fc(piece):
         for index, peer in enumerate(across):
@@ -320,6 +326,44 @@
         for index, peer in enumerate(across):
             fc_over(piece, peer, index, peer).wait_recv()
             fc_near(piece, peer).start()
+
+    def tail_ref(owner):
+        first, stop = pieces[lifted][1], pieces[lifted + 1][2]
+        return fc_ref.at[owner, n_mem - 1, pl.ds(first, stop - first)]
+
+    def lift_out():
+        fc_copy(lifted, me, lift_sem.at[0], sibling).start()
+        fc_copy(lifted + 1, me, lift_sem.at[0], sibling).start()
+
+    def tail_over():
+        own_fc(lifted)
+        own_fc(lifted + 1)
+
+    def tail_relay():
+        for index, peer in enumerate(across):
+            drain(tail_ref(peer), fc_across.at[lifted - 2, index])
+            fc_near(lifted, peer).start()
+            fc_near(lifted + 1, peer).start()
+
+    def lift_over():
+        drain(tail_ref(sibling), lift_sem.at[0])
+        for index, peer in enumerate(across):
+            where = n_y - 2 - index
+            fc_copy(lifted, sibling, fc_across.at[lifted - 1, where], peer).start()
+            fc_copy(lifted + 1, sibling, fc_across.at[lifted, where], peer).start()
+            partner = peer + (1 - 2 * core)
+            fc_copy(lifted + 1, sibling, fc_unit.at[1], partner).start()
+
+    def lift_relay():
+        for index, peer in enumerate(across):
+            partner = peer + (1 - 2 * core)
+            drain(piece_ref(lifted, partner), fc_across.at[lifted - 1, index])
+            fc_near(lifted, partner).start()
+
+    def lift_end():
+        for index, peer in enumerate(across):
+            partner = peer + (1 - 2 * core)
+            drain(piece_ref(lifted + 1, partner), fc_across.at[lifted, index])
 
     def seen_copy(h, target):
         ref = seen_ref.at[me, h]
@@ -438,6 +482,10 @@
     def _():
         admit()
 
+    @pl.when(core == 0)
+    def _():
+        lift_out()
+
     share = slots // CHUNKS
     width = min(share, 512)
     flat = jnp.concatenate(
@@ -466,9 +514,9 @@
                 meet_tiles()
 
     near_seen()
-    n_pieces = len(pieces)
-    for piece in range(3, n_pieces - 1):
+    for piece in range(3, lifted):
         own_fc(piece)
+
 
     @pl.when(wraps)
     def _():
@@ -624,7 +672,11 @@
             t_recv.at[0],
             {"mem": target},
         ).start()
-    finish_fc(n_pieces - 1)
+    @pl.when(core != 0)
+    def _():
+        tail_over()
+        lift_over()
+
     trecv_ref[me] = tsend_ref[me]
 
     group = 8
@@ -653,18 +705,38 @@
         moved = jnp.transpose(moved_ref[block, start:stop], (1, 0, 2)).astype(jnp.bfloat16)
         out_ref[:, start:stop, where] = moved
 
-    for piece in range(4, n_pieces - 1):
+    for piece in range(4, lifted):
         relay_fc(piece)
 
+    @pl.when(core != 0)
+    def _():
+        tail_relay()
+
     drain(trecv_ref.at[pl.ds(0, n_mem - 1)], t_recv.at[0])
 
-    n_units = len(units)
-    for chosen in (range(n_units - 2), range(n_units - 2, n_units - 1), range(n_units - 1, n_units)):
-        rows = sum(units[unit][2] - units[unit][1] for unit in chosen)
-        owners = n_y if chosen[-1] < n_units - 1 else n_mem - 1
-        count(2 * owners * rows * members * wide, fc_unit.at[chosen[-1] + 3 - n_units])
-        for unit in chosen:
-            apply(*units[unit])
+    @pl.when(core != 0)
+    def _():
+        lift_relay()
+
+    count(2 * n_y * fields * (n_mem - 1) * members * wide, fc_unit.at[0])
+
+    for unit in units[:-2]:
+        apply(*unit)
+
+    count(2 * n_y * (units[-2][2] - units[-2][1]) * members * wide, fc_unit.at[2])
+
+    apply(*units[-2])
+
+    @pl.when(core == 0)
+    def _():
+        last_rows = units[-1][2] - units[-1][1]
+        count(2 * (n_mem - 1) * last_rows * members * wide, fc_unit.at[1])
+
+    @pl.when(core != 0)
+    def _():
+        lift_end()
+
+    apply(*units[-1])
 
     kinds = [fc_ref.at[0], seen_ref.at[0], part_ref, stage_ref.at[:, :, 0], tsend_ref.at[0]]
     sizes = [ref.dtype.itemsize * math.prod(ref.shape) for ref in kinds]
@@ -672,7 +744,16 @@
     total = sum(size * count for size, count in zip(sizes, counts))
     total += sizes[1] // CORES
     total += (sizes[2] + sizes[3] * CORES) * (CORES * near - 1) // (CORES * near)
-    count(total, out_sem.at[0])
+    size = 2 * members * wide * (units[-1][2] - units[-1][1])
+    total -= (n_mem - 1) * size
+
+    @pl.when(core == 0)
+    def _():
+        count(total + size, out_sem.at[0])
+
+    @pl.when(core != 0)
+    def _():
+        count(total + (1 + 4 * (n_y - 1)) * size, out_sem.at[0])
 
 
 def on_device(
@@ -696,11 +777,12 @@
     n_y = n_mem // CORES
     wide = columns // n_mem
     units = [(block, 0, fields) for block in range(n_mem - 1)]
-    cuts = (0, fields - 16, fields - 4, fields)
+    cuts = (0, fields - 12, fields)
     units += [(n_mem - 1, *ends) for ends in zip(cuts[:-1], cuts[1:])]
-    pieces = [(0, 0, 16, 0), (0, 16, 28, 0), (0, 28, 32, 0), (0, 32, fields, 0)]
-    pieces += [(*unit, index) for index, unit in enumerate(units) if index]
-    spare = 8 * everyone * fields * columns
+    pieces = [(0, 0, 8, 0), (0, 8, 28, 0), (0, 28, 32, 0), (0, 32, fields, 0)]
+    pieces += [(*unit, index) for index, unit in enumerate(units[:-1]) if index]
+    pieces += [(n_mem - 1, fields - 12, fields - 4, n_mem), (n_mem - 1, fields - 4, fields, n_mem)]
+    spare = 4 * everyone * fields * columns
     row = lambda a: a.reshape(1, -1)
     table = (CHUNKS // CORES, CORES, slots // CHUNKS // 128, 128)
     far = pl.BlockSpec(memory_space=pltpu.HBM)
@@ -737,8 +819,9 @@
             dma((2,)),
             dma((1,)),
             dma((CHUNKS // CORES,)),
-            dma((len(pieces) - 3, n_y - 1)),
+            dma((len(pieces) - 1, n_y - 1)),
             dma((3,)),
+            dma((1,)),
             dma((2,)),
             dma((1,)),
             pltpu.SemaphoreType.REGULAR,

time: 24.1 us -> 23.7 us (0.983)
    pallas_call x1, Pallas kernels: 23 us -> 22.8 us  [on_device(): pl.pallas_call(functools.partial(kernel, n_mem, n_tile, pieces, units), o...]
where the time goes in v5:
time: 23.7 us; the launch traced here: 23.6 us
  Pallas kernels  22.8 us (96%)
  local copies, waits for them, and re-layouts  0.84 us (4%)
    pallas_call x1, Pallas kernels, on_device(): pl.pallas_call(functools.partial(kernel, n_mem, n_tile, pieces, units), o...  22.8 us
    unnamed x1, local copies, waits for them, and re-layouts  0.84 us

profile of v5, /device:TPU:0, one launch (start us, length us, event | category | flops | bytes accessed | tf_op | source)
XLA Modules:
  0.0 23.6 jit_solution(13843365929034352718)
XLA Ops:
  0.0 22.8 %shard_map.100 = bf16[16,40,512]{2,1,0:T(8,128)(2,1)S(1)} custom-call(bf16[16,40,512]{2,1,0:T(8,128)(2,1)} %ens_hbm.1, f32[1,512]{1,0:T(1,128)} %bitcast.14, f32[16,512]{1,0:T(8,128)} %surf_hbm.1, s32[1,512]{1,0:T(1,128)} %bitcast.15, s32[1,4096]{1,0:T(1,128)} %bitcast.9, s32[1,4096]{1,0:T(1,128)} %bitcast.10, s32[2,2,8,128]{3,2,1,0:T(8,128)} %bitcast.11, ...), custom_call_target="tpu_custom_call" | custom-call | tf_op jit(solution)/shard_map/pallas_call | solution.py:790
  22.8 0.8 %copy.12 = bf16[16,40,512]{2,1,0:T(8,128)(2,1)} copy(bf16[16,40,512]{2,1,0:T(8,128)(2,1)S(1)} %shard_map.100) | data formatting | bytes 1310720

commit v6 on v5

--- a/solution.py
+++ b/solution.py
@@ -212,6 +212,7 @@
     got_ref,
     tsend_ref,
     trecv_ref,
+    left_ref,
     moved_ref,
     bytes_ref,
     ens_sem,
@@ -258,11 +259,11 @@
                 barrier, inc=1, device_id={"mem": GATE, "tile": there}, device_id_type=MESH
             )
 
-    def ens_copy(step):
-        where = pl.ds(pl.multiple_of(step * wide, wide), wide)
-        return pltpu.make_async_copy(
-            ens_hbm.at[:, :, where], ens_ref.at[:, :, where], ens_sem.at[min(step, 1)]
-        )
+    opening = pieces[0][2] + 8
+
+    def ens_copy(step, rows, sem):
+        where = (slice(None), pl.ds(*rows), pl.ds(step * wide, wide))
+        return pltpu.make_async_copy(ens_hbm.at[where], ens_ref.at[where], ens_sem.at[sem])
 
     groups = [
         [(mix_hbm, mix_ref), (surf_hbm, surf_ref), (land_hbm, land_ref)],
@@ -278,11 +279,13 @@
         [pltpu.make_async_copy(src, dst, in_sem.at[min(g, 1)]) for src, dst in group]
         for g, group in enumerate(groups)
     ]
-    ens_copy(0).start()
+    first_load = ens_copy(0, (0, opening), 0)
+    first_load.start()
     for copy in loads[0]:
         copy.start()
+    ens_copy(0, (opening, fields - opening), 1).start()
     for step in range(1, n_mem):
-        ens_copy(step).start()
+        ens_copy(step, (0, fields), 2).start()
     for group in loads[1:]:
         for copy in group:
             copy.start()
@@ -444,7 +447,7 @@
         enter()
 
     head = pieces[0][2]
-    ens_copy(0).wait()
+    first_load.wait()
     count(4 * columns * (members + 2), in_sem.at[0])
     mix_part(0, 0, head)
 
@@ -456,13 +459,14 @@
     def _():
         own_fc(0)
 
+    count(2 * members * wide * (fields - opening), ens_sem.at[1])
     mix_part(0, head, fields)
 
     @pl.when(me != GATE)
     def _():
         own_fc(1)
 
-    count(2 * members * fields * wide * (n_mem - 1), ens_sem.at[1])
+    count(2 * members * wide * fields * (n_mem - 1), ens_sem.at[2])
 
     def mix(step, carry):
         mix_part(step, 0, fields)
@@ -659,9 +663,10 @@
     weight_sum = jnp.sum(drawn[:1] * drawn[8:9], axis=1, keepdims=True) / scale
     turned = root / jnp.sqrt(scale) + mean_weight
     turned = turned + (1.0 - sums / jnp.sqrt(scale) - weight_sum) / everyone
+    rounded = turned.astype(jnp.bfloat16).astype(jnp.float32)
+    turned = jnp.concatenate([rounded, turned - rounded], axis=1).astype(jnp.bfloat16)
     for m in range(n_mem):
-        tsend_ref[m, :, :everyone] = turned[m * members : (m + 1) * members]
-        tsend_ref[m, :, everyone:] = jnp.zeros((members, everyone), jnp.float32)
+        tsend_ref[m] = turned[m * members : (m + 1) * members]
 
     for step in range(1, n_mem):
         target = lax.rem(me + step, n_mem)
@@ -683,7 +688,7 @@
 
     def apply(block, start, stop):
         where = pl.ds(block * wide, wide)
-        left = jnp.concatenate(halves(trecv_ref[block][:, :everyone]), axis=0)
+        left = left_ref[block]
         land = jnp.broadcast_to(land_ref[:, where], (members, wide)) > 0
         for first in range(start, stop, group):
             end = min(first + group, stop)
@@ -713,6 +718,10 @@
         tail_relay()
 
     drain(trecv_ref.at[pl.ds(0, n_mem - 1)], t_recv.at[0])
+    for block in range(n_mem):
+        left = trecv_ref[block].astype(jnp.float32)
+        left = jnp.concatenate([left[:, :everyone], left[:, everyone:]], axis=0)
+        left_ref[block] = left.astype(jnp.bfloat16)
 
     @pl.when(core != 0)
     def _():
@@ -754,6 +763,15 @@
     @pl.when(core != 0)
     def _():
         count(total + (1 + 4 * (n_y - 1)) * size, out_sem.at[0])
+
+
+def store(held_ref, out_ref, sem):
+    parts = 4
+    rows = held_ref.shape[0] // parts
+    for part in range(parts):
+        where = pl.ds(part * rows, rows)
+        pltpu.make_async_copy(held_ref.at[where], out_ref.at[where], sem.at[0]).start()
+    pltpu.make_async_copy(held_ref, out_ref, sem.at[0]).wait()
 
 
 def on_device(
@@ -779,7 +797,7 @@
     units = [(block, 0, fields) for block in range(n_mem - 1)]
     cuts = (0, fields - 12, fields)
     units += [(n_mem - 1, *ends) for ends in zip(cuts[:-1], cuts[1:])]
-    pieces = [(0, 0, 8, 0), (0, 8, 28, 0), (0, 28, 32, 0), (0, 32, fields, 0)]
+    pieces = [(0, 0, 16, 0), (0, 16, 28, 0), (0, 28, 32, 0), (0, 32, fields, 0)]
     pieces += [(*unit, index) for index, unit in enumerate(units[:-1]) if index]
     pieces += [(n_mem - 1, fields - 12, fields - 4, n_mem), (n_mem - 1, fields - 4, fields, n_mem)]
     spare = 4 * everyone * fields * columns
@@ -787,7 +805,7 @@
     table = (CHUNKS // CORES, CORES, slots // CHUNKS // 128, 128)
     far = pl.BlockSpec(memory_space=pltpu.HBM)
     dma = pltpu.SemaphoreType.DMA
-    return pl.pallas_call(
+    held = pl.pallas_call(
         functools.partial(kernel, n_mem, n_tile, pieces, units),
         out_shape=pltpu.VMEM(ensemble_profiles_before.shape, jnp.bfloat16),
         in_specs=[far] * 10,
@@ -811,11 +829,12 @@
             pltpu.VMEM((CORES * near * everyone, 2 * everyone), jnp.float32),
             pltpu.VMEM((CORES * near, everyone // 2, 2 * everyone), jnp.bfloat16),
             pltpu.VMEM((CORES * near, everyone // 2, 2 * everyone), jnp.bfloat16),
-            pltpu.VMEM((n_mem, members, 2 * everyone), jnp.float32),
-            pltpu.VMEM((n_mem, members, 2 * everyone), jnp.float32),
+            pltpu.VMEM((n_mem, members, 2 * everyone), jnp.bfloat16),
+            pltpu.VMEM((n_mem, members, 2 * everyone), jnp.bfloat16),
+            pltpu.VMEM((n_mem, 2 * members, everyone), jnp.bfloat16),
             pltpu.VMEM((n_mem, fields, members, wide), jnp.float32),
             pltpu.VMEM((spare // 512, 128), jnp.float32),
-            dma((2,)),
+            dma((3,)),
             dma((2,)),
             dma((1,)),
             dma((CHUNKS // CORES,)),
@@ -842,6 +861,14 @@
         obs_error.reshape(table),
         local_weight.reshape(near, *table),
     )
+    return pl.pallas_call(
+        store,
+        out_shape=jax.ShapeDtypeStruct(held.shape, held.dtype),
+        in_specs=[pl.BlockSpec(memory_space=pltpu.VMEM)],
+        out_specs=pl.BlockSpec(memory_space=pltpu.HBM),
+        scratch_shapes=[dma((1,))],
+        compiler_params=pltpu.CompilerParams(vmem_limit_bytes=2_000_000),
+    )(held)
 
 
 def fits(n_mem, n_tile, ensemble, slots):

time: 23.7 us -> 23.6 us (level)
  local copies, waits for them, and re-layouts: 0.84 us -> 0 us
  Pallas kernels: 22.8 us -> 23.4 us
    unnamed x1 -> x0, local copies, waits for them, and re-layouts: 0.84 us -> none
    pallas_call x0 -> x1, Pallas kernels: none -> 0.84 us  [on_device(): pl.pallas_call(store, out_shape=jax.ShapeDtypeStruct(held.shape, held.dty...]
where the time goes in v6:
time: 23.6 us; the launch traced here: 23.4 us
  Pallas kernels  23.4 us (99%)
    pallas_call x1, Pallas kernels, on_device(): pl.pallas_call(functools.partial(kernel, n_mem, n_tile, pieces, units), o...  22.6 us
    pallas_call x1, Pallas kernels, on_device(): pl.pallas_call(store, out_shape=jax.ShapeDtypeStruct(held.shape, held.dty...  0.84 us

profile of v6, /device:TPU:0, one launch (start us, length us, event | category | flops | bytes accessed | tf_op | source)
XLA Modules:
  0.0 23.4 jit_solution(9955587654879760743)
XLA Ops:
  0.0 22.6 %shard_map.100.held_ref = bf16[16,40,512]{2,1,0:T(8,128)(2,1)S(1)} custom-call(bf16[16,40,512]{2,1,0:T(8,128)(2,1)} %ens_hbm.1, f32[1,512]{1,0:T(1,128)} %bitcast.14, f32[16,512]{1,0:T(8,128)} %surf_hbm.1, s32[1,512]{1,0:T(1,128)} %bitcast.15, s32[1,4096]{1,0:T(1,128)} %bitcast.9, s32[1,4096]{1,0:T(1,128)} %bitcast.10, s32[2,2,8,128]{3,2,1,0:T(8,128)} %bitcast.11, ...), custom_call_target="tpu_custom_call" | custom-call | tf_op jit(solution)/shard_map/pallas_call | solution.py:808
  22.6 0.8 %shard_map.101 = bf16[16,40,512]{2,1,0:T(8,128)(2,1)} custom-call(bf16[16,40,512]{2,1,0:T(8,128)(2,1)S(1)} %shard_map.100.held_ref), custom_call_target="tpu_custom_call" | custom-call | tf_op jit(solution)/shard_map/pallas_call | solution.py:864

commit v7 on v6

--- a/solution.py
+++ b/solution.py
@@ -797,7 +797,7 @@
     units = [(block, 0, fields) for block in range(n_mem - 1)]
     cuts = (0, fields - 12, fields)
     units += [(n_mem - 1, *ends) for ends in zip(cuts[:-1], cuts[1:])]
-    pieces = [(0, 0, 16, 0), (0, 16, 28, 0), (0, 28, 32, 0), (0, 32, fields, 0)]
+    pieces = [(0, 0, 16, 0), (0, 16, 32, 0), (0, 32, 36, 0), (0, 36, fields, 0)]
     pieces += [(*unit, index) for index, unit in enumerate(units[:-1]) if index]
     pieces += [(n_mem - 1, fields - 12, fields - 4, n_mem), (n_mem - 1, fields - 4, fields, n_mem)]
     spare = 4 * everyone * fields * columns

time: 23.6 us -> 23.6 us (level)
  no operation moved by 1% of the time
where the time goes in v7:
time: 23.6 us; the launch traced here: 23.4 us
  Pallas kernels  23.4 us (99%)
    pallas_call x1, Pallas kernels, on_device(): pl.pallas_call(functools.partial(kernel, n_mem, n_tile, pieces, units), o...  22.6 us
    pallas_call x1, Pallas kernels, on_device(): pl.pallas_call(store, out_shape=jax.ShapeDtypeStruct(held.shape, held.dty...  0.84 us

profile of v7, /device:TPU:0, one launch (start us, length us, event | category | flops | bytes accessed | tf_op | source)
XLA Modules:
  0.0 23.4 jit_solution(11680948015229413071)
XLA Ops:
  0.0 22.6 %shard_map.100.held_ref = bf16[16,40,512]{2,1,0:T(8,128)(2,1)S(1)} custom-call(bf16[16,40,512]{2,1,0:T(8,128)(2,1)} %ens_hbm.1, f32[1,512]{1,0:T(1,128)} %bitcast.14, f32[16,512]{1,0:T(8,128)} %surf_hbm.1, s32[1,512]{1,0:T(1,128)} %bitcast.15, s32[1,4096]{1,0:T(1,128)} %bitcast.9, s32[1,4096]{1,0:T(1,128)} %bitcast.10, s32[2,2,8,128]{3,2,1,0:T(8,128)} %bitcast.11, ...), custom_call_target="tpu_custom_call" | custom-call | tf_op jit(solution)/shard_map/pallas_call | solution.py:808
  22.6 0.8 %shard_map.101 = bf16[16,40,512]{2,1,0:T(8,128)(2,1)} custom-call(bf16[16,40,512]{2,1,0:T(8,128)(2,1)S(1)} %shard_map.100.held_ref), custom_call_target="tpu_custom_call" | custom-call | tf_op jit(solution)/shard_map/pallas_call | solution.py:864
